TPU v7x, 256 devices: a whole 4x4x8 slice. The times are simulated.
256 devices in a mesh: date: 64 (over z_hi, x, y), az: 4 (over z_lo, core).
Axes of the slice: x: 4, y: 4, z: 8 (z_hi: 4, z_lo: 2; z = z_hi * 2 + z_lo), core: 2. Of those that a mesh axis runs over, the one named last changes fastest.
Arguments:
- slc: bfloat16 [128, 2, 256, 3072], P('date', None, 'az'), may hold values from -12 to 12
- az_shift: int32 [128], P('date'), may hold values from -4 to 4, as said below
- rg_shift: int32 [128], P('date'), may hold values from -4 to 4, as said below
- az_frac: int32 [128], P('date'), may hold values from 0 to 15
- rg_frac: int32 [128], P('date'), may hold values from 0 to 15
Outputs:
- coherence: bfloat16 [192, 64, 2, 128], P('date', 'az')
- mean_coherence: float32 [192, 64], P('date', 'az')
Inputs may be any that keep to these rules, and one draw needn't show every extreme that they name: `az_shift`: date 0 has offset 0; some date has offset 4 and some -4. `rg_shift`: date 0 has offset 0; some date has offset 4 and some -4.
All inputs are finite; a program needn't handle non-finite values.
Results may differ from a plain program's by a relative error of at most 0.0035.
Values may be sent and summed in bfloat16 or wider, within the bound.
No kernel may reach another device: no remote copies, remote signals or barrier semaphores. Data moves between devices by JAX's collectives and lax.ppermute only.
A program may use at most 64 MiB of HBM per device.

v0:
```python
import functools

import jax
import jax.numpy as jnp
import numpy as np
from jax import lax
from jax.experimental import pallas as pl
from jax.experimental.pallas import tpu as pltpu
from jax.sharding import PartitionSpec as P


TAPS = 8
KBANK = 16
LOOK_AZ = 4
LOOK_RG = 16
RADIUS = 3
EPS = 1e-06
ROWS = 64
COLS = 3072
TILE = 256
NT = COLS // TILE
LOOKS = ROWS // LOOK_AZ
LCOLS = COLS // LOOK_RG
F32 = jnp.float32
BF16 = jnp.bfloat16
VMEM = pltpu.VMEM
SMEM = pltpu.SMEM

GRANT = pltpu.CompilerParams(vmem_limit_bytes=20 * 2**20)


def kernel_bank():
    fraction = np.arange(KBANK)[:, None] / KBANK
    offset = np.arange(TAPS)[None, :] - (TAPS // 2 - 1) - fraction
    shaped = np.sinc(offset) * (0.5 + 0.5 * np.cos(np.pi * offset / (TAPS // 2 + 0.5)))
    return (shaped / shaped.sum(axis=1, keepdims=True)).astype(np.float32)


def iota(shape, dim):
    return lax.broadcasted_iota(jnp.int32, shape, dim)


def near(*arrays):
    return [pltpu.with_memory_space_constraint(a, VMEM) for a in arrays]


def two_halves(value):
    high = value.astype(BF16)
    return high, (value - high.astype(F32)).astype(BF16)


def dot(a, b, dims=((1,), (0,))):
    return lax.dot_general(a, b, (dims, ((), ())), preferred_element_type=F32)


def band(tap_of, weight):
    total = jnp.zeros(tap_of.shape, F32)
    for tap in range(TAPS):
        total = jnp.where(tap_of == tap, weight(tap), total)
    return two_halves(total)


def resample_kernel(
    date, azs, rgs, azf, rgf, bank, own, before, after, out, rows_in, wide_hi, wide_lo, arrived
):
    copies = [
        pltpu.make_async_copy(own.at[date, part], rows_in.at[part, 0:ROWS], arrived.at[part])
        for part in range(2)
    ]
    for copy in copies:
        copy.start()
    source = iota((ROWS, ROWS + 16), 1)
    source = jnp.where(
        source < ROWS, source, jnp.where(source < ROWS + 8, source - ROWS - 8, source - 8)
    )
    az_frac = azf[date]
    rg_frac = rgf[date]
    az_hi, az_lo = band(
        source - iota((ROWS, ROWS + 16), 0) - azs[date] + (TAPS // 2 - 1),
        lambda tap: bank[az_frac, tap],
    )
    az_both = jnp.concatenate([az_hi, az_lo], axis=0)
    half = TILE // 2
    rg_hi, rg_lo = band(
        iota((2 * TILE, TILE), 0) - half - iota((2 * TILE, TILE), 1) - rgs[date] + (TAPS // 2 - 1),
        lambda tap: bank[rg_frac, tap],
    )
    blank = jnp.zeros((ROWS, half), BF16)
    for part in range(2):
        rows_in[part, ROWS : ROWS + 16] = jnp.concatenate(
            [before[date, part].astype(F32), after[date, part].astype(F32)], axis=0
        ).astype(BF16)
        copies[part].wait()
        for tile in range(NT + 1):
            first = max(tile * TILE - half, 0)
            last = min(tile * TILE + half, COLS)
            both = dot(az_both, rows_in[part, :, first:last])
            pieces = two_halves(both[:ROWS] + both[ROWS:])
            for piece, wide in zip(pieces, (wide_hi, wide_lo)):
                if tile == 0:
                    piece = jnp.concatenate([blank, piece], axis=1)
                if tile == NT:
                    piece = jnp.concatenate([piece, blank], axis=1)
                place = part * ROWS
                if tile < NT:
                    at = tile * 2 * ROWS + place
                    wide[at : at + ROWS, 0:TILE] = piece
                if tile > 0:
                    at = (tile - 1) * 2 * ROWS + place
                    wide[at : at + ROWS, TILE : 2 * TILE] = piece
    out[...] = dot(wide_hi[...], rg_hi) + (dot(wide_lo[...], rg_hi) + dot(wide_hi[...], rg_lo))


def resample(date, scalars, slc, before, after):
    return pl.pallas_call(
        functools.partial(resample_kernel, date),
        compiler_params=GRANT,
        out_shape=VMEM((NT * 2 * ROWS, TILE), F32),
        in_specs=[pl.BlockSpec(memory_space=SMEM)] * 5
        + [pl.BlockSpec(memory_space=pl.ANY)]
        + [pl.BlockSpec(memory_space=VMEM)] * 2,
        out_specs=pl.BlockSpec(memory_space=VMEM),
        scratch_shapes=[
            pltpu.VMEM((2, ROWS + 16, COLS), BF16),
            pltpu.VMEM((NT * 2 * ROWS, 2 * TILE), BF16),
            pltpu.VMEM((NT * 2 * ROWS, 2 * TILE), BF16),
            pltpu.SemaphoreType.DMA((2,)),
        ],
        cost_estimate=pl.CostEstimate(
            flops=3_000_000_000, transcendentals=0, bytes_accessed=1_600_000
        ),
    )(*scalars, slc, *near(before, after))


def looks_kernel(center, first, second, out, columns):
    columns[...] = jnp.zeros(columns.shape, F32)
    reach = iota((32, TILE), 1) // LOOK_RG + 8 - iota((32, TILE), 0)
    box = jnp.where(jnp.abs(reach) <= RADIUS, 1.0, 0.0).astype(BF16)
    for tile in range(NT):
        at = tile * TILE
        e0 = center[0:8, :, at : at + TILE].astype(F32).reshape(ROWS, TILE)
        e1 = center[8:16, :, at : at + TILE].astype(F32).reshape(ROWS, TILE)
        cross = []
        power = []
        for stack in (first, second):
            s0 = stack[tile * 2 * ROWS : tile * 2 * ROWS + ROWS]
            s1 = stack[tile * 2 * ROWS + ROWS : (tile + 1) * 2 * ROWS]
            cross.append(e0 * s0 + e1 * s1)
            cross.append(e1 * s0 - e0 * s1)
            power.append(s0 * s0 + s1 * s1)
        power.append(e0 * e0 + e1 * e1)
        high, low = two_halves(jnp.concatenate(cross + power, axis=0))
        nt = ((1,), (1,))
        columns[tile * 16 : tile * 16 + 32] += dot(box, high, nt) + dot(box, low, nt)
    quantities = 7
    pixel = iota((quantities * ROWS, 128), 0)
    box_rows = jnp.where(pixel // LOOK_AZ == iota((quantities * ROWS, 128), 1), 1.0 / 64, 0.0)
    box_rows = box_rows.astype(BF16)
    high, low = two_halves(columns[8 : 8 + LCOLS])
    out[...] = dot(high, box_rows) + dot(low, box_rows)


def looks(center, first, second):
    return pl.pallas_call(
        looks_kernel,
        name="looks",
        compiler_params=GRANT,
        out_shape=VMEM((LCOLS, 128), F32),
        in_specs=[pl.BlockSpec(memory_space=VMEM)] * 3,
        out_specs=pl.BlockSpec(memory_space=VMEM),
        scratch_shapes=[pltpu.VMEM((LCOLS + 16, 7 * ROWS), F32)],
    )(*near(center, first, second))


def coherence_kernel(own, before, after, out, kept):
    source = iota((384, 384), 0)
    target = iota((384, 384), 1)
    row_in = source % 16 + (source // 128) * 16 - 16
    lane = source % 128
    quantity = lane // 16
    group = target // 128
    slot = target % 128
    date = slot // 32
    wanted = jnp.where(
        group == 0, date * 2 + slot % 2, jnp.where(group == 1, 4 + date, 6)
    )
    reach = row_in - (slot % 32) // 2
    hit = (quantity == wanted) & (jnp.abs(reach) <= RADIUS) & (slot < 64)
    box = jnp.where(hit, 1.0, 0.0).astype(BF16)
    high, low = two_halves(jnp.concatenate([before[...], own[...], after[...]], axis=1))
    summed = dot(high, box) + dot(low, box)
    cross = summed[:, 0:128]
    scale = 1.0 / jnp.sqrt(summed[:, 256:384] * summed[:, 128:256] + EPS)
    kept[...] = cross * scale
    third = LCOLS // 3
    pieces = [kept[pl.ds(k, third, stride=3), :] for k in range(3)]
    pair = jnp.concatenate([pieces[0][:, 0:64], pieces[1][:, 0:64]], axis=1)
    out[...] = jnp.stack([pair, pieces[2]], axis=1).astype(BF16)


def coherence(own, before, after):
    return pl.pallas_call(
        coherence_kernel,
        name="coherence",
        compiler_params=GRANT,
        out_shape=VMEM((LCOLS // 3, 2, 128), BF16),
        in_specs=[pl.BlockSpec(memory_space=VMEM)] * 3,
        out_specs=pl.BlockSpec(memory_space=VMEM),
        scratch_shapes=[pltpu.VMEM((LCOLS, 128), F32)],
    )(*near(own, before, after))


def finish_kernel(arrived, out, mean):
    source = iota((64, 128), 0)
    lane = iota((64, 128), 1)
    tn = ((0,), (0,))
    wide = arrived[...].astype(F32)
    packed = jnp.concatenate([wide[:, 0], wide[:, 1, 0:64]], axis=1).astype(BF16)
    placed = []
    for date in range(2):
        spread = jnp.where(lane == source * 2 + date, 1.0, 0.0).astype(BF16)
        placed.append(dot(packed, spread, tn))
    rows = jnp.concatenate(
        [placed[0][k * 64 : k * 64 + 32] + placed[1][k * 64 + 32 : k * 64 + 64] for k in range(3)],
        axis=0,
    )
    out[...] = rows.astype(BF16)
    square = rows * rows
    pair = jnp.where(iota((48, 96), 1) // 2 == iota((48, 96), 0), 1.0, 0.0)
    exact = lax.Precision.HIGHEST
    magnitude = jnp.sqrt(jnp.dot(pair, square, precision=exact, preferred_element_type=F32))
    share = jnp.full((8, 128), 1.0 / 128, F32)
    average = lax.dot_general(
        share, magnitude, (((1,), (1,)), ((), ())), precision=exact, preferred_element_type=F32
    )
    for k in range(3):
        mean[k : k + 1] = average[0:1, k * LOOKS : (k + 1) * LOOKS]


def finish(arrived):
    return pl.pallas_call(
        finish_kernel,
        name="finish",
        compiler_params=GRANT,
        out_shape=(
            jax.ShapeDtypeStruct((96, 128), BF16),
            jax.ShapeDtypeStruct((3, LOOKS), F32),
        ),
        in_specs=[pl.BlockSpec(memory_space=VMEM)],
        out_specs=(pl.BlockSpec(memory_space=VMEM), pl.BlockSpec(memory_space=VMEM)),
    )(*near(arrived))


def place(z, x, y):
    return z * 16 + x * 4 + y


HOMES = (
    ((0, 0), (0, 3), (1, 3), (3, 3)),
    ((1, 0), (2, 0), (1, 1), (2, 1)),
    ((3, 0), (3, 1), (3, 2), (2, 3)),
    ((0, 1), (0, 2), (1, 2), (2, 2)),
)


def body(slc, az_shift, rg_shift, az_frac, rg_frac):
    up = [(i, i + 1) for i in range(3)]
    down = [(i + 1, i) for i in range(3)]
    scalars = (az_shift, rg_shift, az_frac, rg_frac, jnp.asarray(kernel_bank()))
    quarters = [
        slc[0, part, 32 * half : 32 * half + 32].reshape(4, 8, COLS)
        for part in range(2)
        for half in range(2)
    ]

    first = lax.axis_index("date") == 0
    pieces = [lax.ppermute(quarters[k], "date", [(0, place(0, *HOMES[k][0]))]) for k in range(1, 4)]
    before = lax.ppermute(slc[:, :, ROWS - 8 :], "az", up)
    after = lax.ppermute(slc[:, :, :8], "az", down)
    pieces, before, after = lax.optimization_barrier((pieces, before, after))
    quarter = jnp.where(first, quarters[0], jnp.zeros_like(quarters[0])) + sum(pieces)

    pieces = [
        lax.ppermute(
            quarter[k : k + 1],
            "date",
            [(place(0, *homes[0]), place(0, *homes[k])) for homes in HOMES],
        )
        for k in range(1, 4)
    ]
    early = resample(0, scalars, slc, before, after)
    pieces, early = lax.optimization_barrier((pieces, early))
    chunk = quarter[0:1] + sum(pieces)

    flat = [home for homes in HOMES for home in homes]
    pieces = [
        lax.ppermute(chunk, "date", [(place(0, *home), place(k, *home)) for home in flat])
        for k in (2, 1, 3)
    ]
    late = resample(1, scalars, slc, before, after)
    pieces, late = lax.optimization_barrier((pieces, late))
    whole = chunk + sum(pieces)

    planes = [[place(z, *home) for home in flat] for z in range(4)]
    copies = jnp.broadcast_to(whole, (16,) + whole.shape[1:])
    center = lax.all_to_all(copies, "date", 0, 0, axis_index_groups=planes, tiled=True)
    own = looks(center, early, late)
    outgoing = coherence(own, lax.ppermute(own, "az", up), lax.ppermute(own, "az", down))
    arrived = lax.all_to_all(outgoing, "date", split_axis=0, concat_axis=0, tiled=True)
    rows, mean = finish(arrived)
    return rows.reshape(3, LOOKS, 2, 128), mean


def solution(mesh):
    placed = (P("date", None, "az", None), P("date"), P("date"), P("date"), P("date"))
    return jax.shard_map(
        body,
        mesh=mesh,
        in_specs=placed,
        out_specs=(P("date", "az", None, None), P("date", "az")),
        check_vma=False,
    )
```

profile of v0, /device:TPU:32, one launch (start us, length us, event | category | flops | bytes accessed | tf_op | source)
XLA Modules:
  0.0 83.3 jit_solution(808259053829074088)
XLA Ops:
  0.7 1.8 %fusion = (bf16[2,2,8,3072]{3,2,1,0:T(8,128)(2,1)}, bf16[2,2,8,3072]{3,2,1,0:T(8,128)(2,1)S(1)}) fusion(bf16[2,2,64,3072]{3,2,1,0:T(8,128)(2,1)} %own.3), kind=kLoop, calls=%fused_computation.6 | loop fusion | bytes 786432 | tf_op jit(solution)/shard_map/slice | solution.py:279
  2.5 1.9 %collective-permute-start.4 = (bf16[2,2,8,3072]{3,2,1,0:T(8,128)(2,1)}, bf16[2,2,8,3072]{3,2,1,0:T(8,128)(2,1)S(1)}, u32[]{:S(2)}, u32[]{:S(2)}) collective-permute-start(bf16[2,2,8,3072]{3,2,1,0:T(8,128)(2,1)} %get-tuple-element.32), channel_id=1, source_target_pairs={{1,0},{2,1},{3,2},{5,4},{6,5},{7,6},{9,8},{10,9},{11,10},{13,12},{... | collective-permute-start | bytes 589832 | tf_op jit(solution)/shard_map/ppermute | solution.py:279
  4.4 2.4 %collective-permute-start.3 = (bf16[2,2,8,3072]{3,2,1,0:T(8,128)(2,1)S(1)}, bf16[2,2,8,3072]{3,2,1,0:T(8,128)(2,1)S(1)}, u32[]{:S(2)}, u32[]{:S(2)}) collective-permute-start(bf16[2,2,8,3072]{3,2,1,0:T(8,128)(2,1)S(1)} %get-tuple-element.33), channel_id=1, source_target_pairs={{0,1},{1,2},{2,3},{4,5},{5,6},{6,7},{8,9},{9,10},{10,11},{12,13},{... | collective-permute-start | bytes 589832 | tf_op jit(solution)/shard_map/ppermute | solution.py:278
  6.9 1.2 %slice_bitcast_fusion = (bf16[4,8,3072]{2,1,0:T(8,128)(2,1)S(1)}, bf16[4,8,3072]{2,1,0:T(8,128)(2,1)S(1)}, bf16[4,8,3072]{2,1,0:T(8,128)(2,1)S(1)}) fusion(bf16[2,2,64,3072]{3,2,1,0:T(8,128)(2,1)} %own.3), kind=kLoop, calls=%fused_computation.1 | loop fusion | bytes 1179648 | tf_op jit(solution)/shard_map/reshape;squeeze | solution.py:271
  8.0 3.5 %collective-permute-start.2 = (bf16[4,8,3072]{2,1,0:T(8,128)(2,1)S(1)}, bf16[4,8,3072]{2,1,0:T(8,128)(2,1)S(1)}, u32[]{:S(2)}, u32[]{:S(2)}) collective-permute-start(bf16[4,8,3072]{2,1,0:T(8,128)(2,1)S(1)} %get-tuple-element.34), channel_id=1, source_target_pairs={{0,4},{1,5},{2,6},{3,7}} | collective-permute-start | bytes 589832 | tf_op jit(solution)/shard_map/ppermute | solution.py:277
  11.5 1.9 %collective-permute-start.1 = (bf16[4,8,3072]{2,1,0:T(8,128)(2,1)S(1)}, bf16[4,8,3072]{2,1,0:T(8,128)(2,1)S(1)}, u32[]{:S(2)}, u32[]{:S(2)}) collective-permute-start(bf16[4,8,3072]{2,1,0:T(8,128)(2,1)S(1)} %get-tuple-element.35), channel_id=1, source_target_pairs={{0,48},{1,49},{2,50},{3,51}} | collective-permute-start | bytes 589832 | tf_op jit(solution)/shard_map/ppermute | solution.py:277
  13.4 1.3 %collective-permute-start = (bf16[4,8,3072]{2,1,0:T(8,128)(2,1)S(1)}, bf16[4,8,3072]{2,1,0:T(8,128)(2,1)S(1)}, u32[]{:S(2)}, u32[]{:S(2)}) collective-permute-start(bf16[4,8,3072]{2,1,0:T(8,128)(2,1)S(1)} %get-tuple-element.36), channel_id=1, source_target_pairs={{0,16},{1,17},{2,18},{3,19}} | collective-permute-start | bytes 589832 | tf_op jit(solution)/shard_map/ppermute | solution.py:277
  15.2 1.9 %collective-permute-done.1 = bf16[4,8,3072]{2,1,0:T(8,128)(2,1)S(1)} collective-permute-done((bf16[4,8,3072]{2,1,0:T(8,128)(2,1)S(1)}, bf16[4,8,3072]{2,1,0:T(8,128)(2,1)S(1)}, u32[]{:S(2)}, u32[]{:S(2)}) %collective-permute-start.1) | collective-permute-done | bytes 196640 | tf_op jit(solution)/shard_map/ppermute | solution.py:277
  17.1 1.3 %collective-permute-done = bf16[4,8,3072]{2,1,0:T(8,128)(2,1)S(1)} collective-permute-done((bf16[4,8,3072]{2,1,0:T(8,128)(2,1)S(1)}, bf16[4,8,3072]{2,1,0:T(8,128)(2,1)S(1)}, u32[]{:S(2)}, u32[]{:S(2)}) %collective-permute-start) | collective-permute-done | bytes 196640 | tf_op jit(solution)/shard_map/ppermute | solution.py:277
  18.5 1.3 %collective-permute-start.7 = (bf16[1,8,3072]{2,1,0:T(8,128)(2,1)S(1)}, bf16[1,8,3072]{2,1,0:T(8,128)(2,1)S(1)}, u32[]{:S(2)}, u32[]{:S(2)}) collective-permute-start(bf16[1,8,3072]{2,1,0:T(8,128)(2,1)S(1)} %get-tuple-element.37), channel_id=1, source_target_pairs={{0,60},{16,36},{48,44},{4,40},{1,61},{17,37},{49,45},{5,41},{2,62}... | collective-permute-start | bytes 147464 | tf_op jit(solution)/shard_map/ppermute | solution.py:284
  19.8 1.3 %collective-permute-start.6 = (bf16[1,8,3072]{2,1,0:T(8,128)(2,1)S(1)}, bf16[1,8,3072]{2,1,0:T(8,128)(2,1)S(1)}, u32[]{:S(2)}, u32[]{:S(2)}) collective-permute-start(bf16[1,8,3072]{2,1,0:T(8,128)(2,1)S(1)} %get-tuple-element.38), channel_id=1, source_target_pairs={{0,28},{16,20},{48,56},{4,24},{1,29},{17,21},{49,57},{5,25},{2,30}... | collective-permute-start | bytes 147464 | tf_op jit(solution)/shard_map/ppermute | solution.py:284
  21.1 1.3 %collective-permute-start.5 = (bf16[1,8,3072]{2,1,0:T(8,128)(2,1)S(1)}, bf16[1,8,3072]{2,1,0:T(8,128)(2,1)S(1)}, u32[]{:S(2)}, u32[]{:S(2)}) collective-permute-start(bf16[1,8,3072]{2,1,0:T(8,128)(2,1)S(1)} %get-tuple-element.39), channel_id=1, source_target_pairs={{0,12},{16,32},{48,52},{4,8},{1,13},{17,33},{49,53},{5,9},{2,14},{... | collective-permute-start | bytes 147464 | tf_op jit(solution)/shard_map/ppermute | solution.py:284
  22.4 3.8 %shard_map.77.first = f32[1536,256]{1,0:T(8,128)S(1)} custom-call(s32[2]{0:T(128)S(1)} %copy-done.1, s32[2]{0:T(128)S(1)} %copy-done.2, s32[2]{0:T(128)S(1)} %copy-done.3, s32[2]{0:T(128)S(1)} %copy-done.4, f32[16,8]{1,0:T(8,128)S(1)} %copy-done.5, bf16[2,2,64,3072]{3,2,1,0:T(8,128)(2,1)S(1)} %copy-done, ...), custom_call_target="tpu_custom_call" | custom-call | flops 3000000000 | bytes 1600000 | tf_op jit(solution)/shard_map/pallas_call | solution.py:115
  26.2 1.3 %collective-permute-start.10 = (bf16[1,8,3072]{2,1,0:T(8,128)(2,1)S(1)}, bf16[1,8,3072]{2,1,0:T(8,128)(2,1)S(1)}, u32[]{:S(2)}, u32[]{:S(2)}) collective-permute-start(bf16[1,8,3072]{2,1,0:T(8,128)(2,1)S(1)} %slice_add_fusion), channel_id=1, source_target_pairs={{0,192},{12,204},{28,220},{60,252},{16,208},{32,224},{20,212},{36,... | collective-permute-start | bytes 147464 | tf_op jit(solution)/shard_map/ppermute | solution.py:297
  27.5 1.3 %collective-permute-start.9 = (bf16[1,8,3072]{2,1,0:T(8,128)(2,1)S(1)}, bf16[1,8,3072]{2,1,0:T(8,128)(2,1)S(1)}, u32[]{:S(2)}, u32[]{:S(2)}) collective-permute-start(bf16[1,8,3072]{2,1,0:T(8,128)(2,1)S(1)} %slice_add_fusion), channel_id=1, source_target_pairs={{0,64},{12,76},{28,92},{60,124},{16,80},{32,96},{20,84},{36,100},{... | collective-permute-start | bytes 147464 | tf_op jit(solution)/shard_map/ppermute | solution.py:297
  28.8 1.3 %collective-permute-start.8 = (bf16[1,8,3072]{2,1,0:T(8,128)(2,1)S(1)}, bf16[1,8,3072]{2,1,0:T(8,128)(2,1)S(1)}, u32[]{:S(2)}, u32[]{:S(2)}) collective-permute-start(bf16[1,8,3072]{2,1,0:T(8,128)(2,1)S(1)} %slice_add_fusion), channel_id=1, source_target_pairs={{0,128},{12,140},{28,156},{60,188},{16,144},{32,160},{20,148},{36,... | collective-permute-start | bytes 147464 | tf_op jit(solution)/shard_map/ppermute | solution.py:297
  30.1 3.8 %shard_map.78.second = f32[1536,256]{1,0:T(8,128)S(1)} custom-call(s32[2]{0:T(128)S(1)} %copy-done.1, s32[2]{0:T(128)S(1)} %copy-done.2, s32[2]{0:T(128)S(1)} %copy-done.3, s32[2]{0:T(128)S(1)} %copy-done.4, f32[16,8]{1,0:T(8,128)S(1)} %copy-done.5, bf16[2,2,64,3072]{3,2,1,0:T(8,128)(2,1)S(1)} %copy-done, ...), custom_call_target="tpu_custom_call" | custom-call | flops 3000000000 | bytes 1600000 | tf_op jit(solution)/shard_map/pallas_call | solution.py:115
  34.0 16.4 %all_to_all.10.center = bf16[16,8,3072]{2,1,0:T(8,128)(2,1)S(1)} all-to-all(bf16[16,8,3072]{2,1,0:T(8,128)(2,1)S(1)} %broadcast_in_dim.12), channel_id=1, replica_groups={{0,12,28,60,16,32,20,36,48,52,56,44,4,8,24,40},{64,76,92,124,80,96,84,1..., dimensions={0} | all-to-all | bytes 1572864 | tf_op jit(solution)/shard_map/all_to_all | solution.py:306
  50.4 1.9 %looks.1.own = f32[192,128]{1,0:T(8,128)S(1)} custom-call(bf16[16,8,3072]{2,1,0:T(8,128)(2,1)S(1)} %all_to_all.10.center, f32[1536,256]{1,0:T(8,128)S(1)} %shard_map.77.first, f32[1536,256]{1,0:T(8,128)S(1)} %shard_map.78.second), custom_call_target="tpu_custom_call" | custom-call | tf_op jit(solution)/shard_map/looks/pallas_call | solution.py:164
  52.3 2.7 %collective-permute-start.12 = (f32[192,128]{1,0:T(8,128)S(1)}, f32[192,128]{1,0:T(8,128)S(1)}, u32[]{:S(2)}, u32[]{:S(2)}) collective-permute-start(f32[192,128]{1,0:T(8,128)S(1)} %looks.1.own), channel_id=1, source_target_pairs={{1,0},{2,1},{3,2},{5,4},{6,5},{7,6},{9,8},{10,9},{11,10},{13,12},{... | collective-permute-start | bytes 294920 | tf_op jit(solution)/shard_map/ppermute | solution.py:308
  55.0 1.9 %collective-permute-start.11 = (f32[192,128]{1,0:T(8,128)S(1)}, f32[192,128]{1,0:T(8,128)S(1)}, u32[]{:S(2)}, u32[]{:S(2)}) collective-permute-start(f32[192,128]{1,0:T(8,128)S(1)} %looks.1.own), channel_id=1, source_target_pairs={{0,1},{1,2},{2,3},{4,5},{5,6},{6,7},{8,9},{9,10},{10,11},{12,13},{... | collective-permute-start | bytes 294920 | tf_op jit(solution)/shard_map/ppermute | solution.py:308
  57.2 4.3 %collective-permute-done.11.before = f32[192,128]{1,0:T(8,128)S(1)} collective-permute-done((f32[192,128]{1,0:T(8,128)S(1)}, f32[192,128]{1,0:T(8,128)S(1)}, u32[]{:S(2)}, u32[]{:S(2)}) %collective-permute-start.11) | collective-permute-done | bytes 98336 | tf_op jit(solution)/shard_map/ppermute | solution.py:308
  62.1 19.9 %all_to_all.11.arrived = bf16[64,2,128]{2,1,0:T(2,128)(2,1)S(1)} all-to-all(bf16[64,2,128]{2,1,0:T(2,128)(2,1)S(1)} %coherence.1), channel_id=1, replica_groups=mesh['date'=64,'az'=4] {'date'}, dimensions={0} | all-to-all | bytes 65536 | tf_op jit(solution)/shard_map/all_to_all | solution.py:309
  82.0 1.3 %finish.1 = (bf16[96,128]{1,0:T(8,128)(2,1)}, f32[3,16]{1,0:T(4,128)}) custom-call(bf16[64,2,128]{2,1,0:T(2,128)(2,1)S(1)} %all_to_all.11.arrived), custom_call_target="tpu_custom_call" | custom-call | tf_op jit(solution)/shard_map/finish/pallas_call | solution.py:241
  (28 shorter events, 1.6 us)
Async XLA Ops:
  0.6 21.7 %copy-start.5 = (f32[16,8]{1,0:T(8,128)S(1)}, f32[16,8]{1,0:T(8,128)}, u32[]{:S(2)}) copy-start(f32[16,8]{1,0:T(8,128)} %constant.12.clone.bank) | copy-start | bytes 1540
  0.6 17.7 %copy-start = (bf16[2,2,64,3072]{3,2,1,0:T(8,128)(2,1)S(1)}, bf16[2,2,64,3072]{3,2,1,0:T(8,128)(2,1)}, u32[]{:S(2)}) copy-start(bf16[2,2,64,3072]{3,2,1,0:T(8,128)(2,1)} %own.3) | copy-start | bytes 4718596
  0.7 21.7 %copy-start.4 = (s32[2]{0:T(128)S(1)}, s32[2]{0:T(128)}, u32[]{:S(2)}) copy-start(s32[2]{0:T(128)} %rgf.3) | copy-start | bytes 28
  0.7 21.7 %copy-start.3 = (s32[2]{0:T(128)S(1)}, s32[2]{0:T(128)}, u32[]{:S(2)}) copy-start(s32[2]{0:T(128)} %azf.3) | copy-start | bytes 28
  0.7 21.7 %copy-start.2 = (s32[2]{0:T(128)S(1)}, s32[2]{0:T(128)}, u32[]{:S(2)}) copy-start(s32[2]{0:T(128)} %rgs.3) | copy-start | bytes 28
  0.7 21.7 %copy-start.1 = (s32[2]{0:T(128)S(1)}, s32[2]{0:T(128)}, u32[]{:S(2)}) copy-start(s32[2]{0:T(128)} %azs.3) | copy-start | bytes 28
  2.5 12.2 %collective-permute-start.4 = (bf16[2,2,8,3072]{3,2,1,0:T(8,128)(2,1)}, bf16[2,2,8,3072]{3,2,1,0:T(8,128)(2,1)S(1)}, u32[]{:S(2)}, u32[]{:S(2)}) collective-permute-start(bf16[2,2,8,3072]{3,2,1,0:T(8,128)(2,1)} %get-tuple-element.32), channel_id=1, source_target_pairs={{1,0},{2,1},{3,2},{5,4},{6,5},{7,6},{9,8},{10,9},{11,10},{13,12},{... | collective-permute-start | bytes 589832 | tf_op jit(solution)/shard_map/ppermute | solution.py:279
  4.4 10.3 %collective-permute-start.3 = (bf16[2,2,8,3072]{3,2,1,0:T(8,128)(2,1)S(1)}, bf16[2,2,8,3072]{3,2,1,0:T(8,128)(2,1)S(1)}, u32[]{:S(2)}, u32[]{:S(2)}) collective-permute-start(bf16[2,2,8,3072]{3,2,1,0:T(8,128)(2,1)S(1)} %get-tuple-element.33), channel_id=1, source_target_pairs={{0,1},{1,2},{2,3},{4,5},{5,6},{6,7},{8,9},{9,10},{10,11},{12,13},{... | collective-permute-start | bytes 589832 | tf_op jit(solution)/shard_map/ppermute | solution.py:278
  8.0 7.2 %collective-permute-start.2 = (bf16[4,8,3072]{2,1,0:T(8,128)(2,1)S(1)}, bf16[4,8,3072]{2,1,0:T(8,128)(2,1)S(1)}, u32[]{:S(2)}, u32[]{:S(2)}) collective-permute-start(bf16[4,8,3072]{2,1,0:T(8,128)(2,1)S(1)} %get-tuple-element.34), channel_id=1, source_target_pairs={{0,4},{1,5},{2,6},{3,7}} | collective-permute-start | bytes 589832 | tf_op jit(solution)/shard_map/ppermute | solution.py:277
  11.5 5.5 %collective-permute-start.1 = (bf16[4,8,3072]{2,1,0:T(8,128)(2,1)S(1)}, bf16[4,8,3072]{2,1,0:T(8,128)(2,1)S(1)}, u32[]{:S(2)}, u32[]{:S(2)}) collective-permute-start(bf16[4,8,3072]{2,1,0:T(8,128)(2,1)S(1)} %get-tuple-element.35), channel_id=1, source_target_pairs={{0,48},{1,49},{2,50},{3,51}} | collective-permute-start | bytes 589832 | tf_op jit(solution)/shard_map/ppermute | solution.py:277
  13.4 5.0 %collective-permute-start = (bf16[4,8,3072]{2,1,0:T(8,128)(2,1)S(1)}, bf16[4,8,3072]{2,1,0:T(8,128)(2,1)S(1)}, u32[]{:S(2)}, u32[]{:S(2)}) collective-permute-start(bf16[4,8,3072]{2,1,0:T(8,128)(2,1)S(1)} %get-tuple-element.36), channel_id=1, source_target_pairs={{0,16},{1,17},{2,18},{3,19}} | collective-permute-start | bytes 589832 | tf_op jit(solution)/shard_map/ppermute | solution.py:277
  18.5 7.7 %collective-permute-start.7 = (bf16[1,8,3072]{2,1,0:T(8,128)(2,1)S(1)}, bf16[1,8,3072]{2,1,0:T(8,128)(2,1)S(1)}, u32[]{:S(2)}, u32[]{:S(2)}) collective-permute-start(bf16[1,8,3072]{2,1,0:T(8,128)(2,1)S(1)} %get-tuple-element.37), channel_id=1, source_target_pairs={{0,60},{16,36},{48,44},{4,40},{1,61},{17,37},{49,45},{5,41},{2,62}... | collective-permute-start | bytes 147464 | tf_op jit(solution)/shard_map/ppermute | solution.py:284
  19.8 6.4 %collective-permute-start.6 = (bf16[1,8,3072]{2,1,0:T(8,128)(2,1)S(1)}, bf16[1,8,3072]{2,1,0:T(8,128)(2,1)S(1)}, u32[]{:S(2)}, u32[]{:S(2)}) collective-permute-start(bf16[1,8,3072]{2,1,0:T(8,128)(2,1)S(1)} %get-tuple-element.38), channel_id=1, source_target_pairs={{0,28},{16,20},{48,56},{4,24},{1,29},{17,21},{49,57},{5,25},{2,30}... | collective-permute-start | bytes 147464 | tf_op jit(solution)/shard_map/ppermute | solution.py:284
  21.1 5.1 %collective-permute-start.5 = (bf16[1,8,3072]{2,1,0:T(8,128)(2,1)S(1)}, bf16[1,8,3072]{2,1,0:T(8,128)(2,1)S(1)}, u32[]{:S(2)}, u32[]{:S(2)}) collective-permute-start(bf16[1,8,3072]{2,1,0:T(8,128)(2,1)S(1)} %get-tuple-element.39), channel_id=1, source_target_pairs={{0,12},{16,32},{48,52},{4,8},{1,13},{17,33},{49,53},{5,9},{2,14},{... | collective-permute-start | bytes 147464 | tf_op jit(solution)/shard_map/ppermute | solution.py:284
  26.2 7.7 %collective-permute-start.10 = (bf16[1,8,3072]{2,1,0:T(8,128)(2,1)S(1)}, bf16[1,8,3072]{2,1,0:T(8,128)(2,1)S(1)}, u32[]{:S(2)}, u32[]{:S(2)}) collective-permute-start(bf16[1,8,3072]{2,1,0:T(8,128)(2,1)S(1)} %slice_add_fusion), channel_id=1, source_target_pairs={{0,192},{12,204},{28,220},{60,252},{16,208},{32,224},{20,212},{36,... | collective-permute-start | bytes 147464 | tf_op jit(solution)/shard_map/ppermute | solution.py:297
  27.5 6.4 %collective-permute-start.9 = (bf16[1,8,3072]{2,1,0:T(8,128)(2,1)S(1)}, bf16[1,8,3072]{2,1,0:T(8,128)(2,1)S(1)}, u32[]{:S(2)}, u32[]{:S(2)}) collective-permute-start(bf16[1,8,3072]{2,1,0:T(8,128)(2,1)S(1)} %slice_add_fusion), channel_id=1, source_target_pairs={{0,64},{12,76},{28,92},{60,124},{16,80},{32,96},{20,84},{36,100},{... | collective-permute-start | bytes 147464 | tf_op jit(solution)/shard_map/ppermute | solution.py:297
  28.8 5.1 %collective-permute-start.8 = (bf16[1,8,3072]{2,1,0:T(8,128)(2,1)S(1)}, bf16[1,8,3072]{2,1,0:T(8,128)(2,1)S(1)}, u32[]{:S(2)}, u32[]{:S(2)}) collective-permute-start(bf16[1,8,3072]{2,1,0:T(8,128)(2,1)S(1)} %slice_add_fusion), channel_id=1, source_target_pairs={{0,128},{12,140},{28,156},{60,188},{16,144},{32,160},{20,148},{36,... | collective-permute-start | bytes 147464 | tf_op jit(solution)/shard_map/ppermute | solution.py:297
  52.3 4.9 %collective-permute-start.12 = (f32[192,128]{1,0:T(8,128)S(1)}, f32[192,128]{1,0:T(8,128)S(1)}, u32[]{:S(2)}, u32[]{:S(2)}) collective-permute-start(f32[192,128]{1,0:T(8,128)S(1)} %looks.1.own), channel_id=1, source_target_pairs={{1,0},{2,1},{3,2},{5,4},{6,5},{7,6},{9,8},{10,9},{11,10},{13,12},{... | collective-permute-start | bytes 294920 | tf_op jit(solution)/shard_map/ppermute | solution.py:308
  55.0 6.5 %collective-permute-start.11 = (f32[192,128]{1,0:T(8,128)S(1)}, f32[192,128]{1,0:T(8,128)S(1)}, u32[]{:S(2)}, u32[]{:S(2)}) collective-permute-start(f32[192,128]{1,0:T(8,128)S(1)} %looks.1.own), channel_id=1, source_target_pairs={{0,1},{1,2},{2,3},{4,5},{5,6},{6,7},{8,9},{9,10},{10,11},{12,13},{... | collective-permute-start | bytes 294920 | tf_op jit(solution)/shard_map/ppermute | solution.py:308
where the time goes:
time: 83.8 us; the launch traced here: 83.3 us
  blocking collectives  36.3 us (43%)
  starting transfers between devices  23.3 us (28%)
  Pallas kernels  11.3 us (13%)
  waiting for transfers between devices  8.27 us (10%)
  local copies, waits for them, and re-layouts  3.1 us (4%)
  between operations  0.96 us (1%)
    all_to_all x1, blocking collectives, body(): lax.all_to_all(outgoing, 'date', split_axis=0, concat_axis=0, tiled=True)  19.9 us
    all_to_all x1, blocking collectives, body(): lax.all_to_all(copies, 'date', 0, 0, axis_index_groups=planes, tiled=True)  16.4 us
    pallas_call x2, Pallas kernels, resample(): pl.pallas_call(functools.partial(resample_kernel, date), compiler_params=...  7.52 us
    ppermute x3, starting transfers between devices, body(): lax.ppermute(quarters[k], 'date', [(0, place(0, *HOMES[k][0]))])  6.65 us
    ppermute x1, waiting for transfers between devices, body(): lax.ppermute(own, 'az', up)  4.33 us
    ppermute x3, starting transfers between devices, body(): lax.ppermute(quarter[k:k + 1], 'date', [(place(0, *homes[0]), place(0, *h...  3.88 us
    ppermute x3, starting transfers between devices, body(): lax.ppermute(chunk, 'date', [(place(0, *home), place(k, *home)) for home...  3.88 us
    ppermute x3, waiting for transfers between devices, body(): lax.ppermute(quarters[k], 'date', [(0, place(0, *HOMES[k][0]))])  3.65 us
  transfers between devices with their start and end apart: 13, of which 5 were waited for; matrix products, arithmetic and copies ran while one was open for 1% of the time, Pallas kernels for 9%

commit v1 on v0

--- a/solution.py
+++ b/solution.py
@@ -44,6 +44,10 @@
     return [pltpu.with_memory_space_constraint(a, VMEM) for a in arrays]
 
 
+def far_away(*arrays):
+    return [pltpu.with_memory_space_constraint(a, pltpu.HBM) for a in arrays]
+
+
 def two_halves(value):
     high = value.astype(BF16)
     return high, (value - high.astype(F32)).astype(BF16)
@@ -60,10 +64,40 @@
     return two_halves(total)
 
 
+def odd_block():
+    return lax.rem(lax.axis_index("az"), 2) == 1
+
+
+def in_order(partner, other):
+    odd = odd_block()
+    return [jnp.where(odd, partner, other), jnp.where(odd, other, partner)]
+
+
+def swapped(to_partner, to_other):
+    return (
+        lax.ppermute(to_partner, "az", [(0, 1), (1, 0), (2, 3), (3, 2)]),
+        lax.ppermute(to_other, "az", [(1, 2), (2, 1)]),
+    )
+
+
 def resample_kernel(
-    date, azs, rgs, azf, rgf, bank, own, before, after, out, rows_in, wide_hi, wide_lo, arrived
+    date,
+    azs,
+    rgs,
+    azf,
+    rgf,
+    bank,
+    own,
+    partner,
+    other,
+    near_out,
+    *rest,
 ):
+    *far_out, power, rows_in, edges, wide_hi, wide_lo, arrived = rest
     copies = [
+        pltpu.make_async_copy(source.at[date], edges.at[at], arrived.at[2 + at])
+        for at, source in enumerate((partner, other))
+    ] + [
         pltpu.make_async_copy(own.at[date, part], rows_in.at[part, 0:ROWS], arrived.at[part])
         for part in range(2)
     ]
@@ -87,10 +121,14 @@
     )
     blank = jnp.zeros((ROWS, half), BF16)
     for part in range(2):
+        if part == 0:
+            copies[0].wait()
+            copies[1].wait()
+        pair = edges[0, part].astype(F32), edges[1, part].astype(F32)
         rows_in[part, ROWS : ROWS + 16] = jnp.concatenate(
-            [before[date, part].astype(F32), after[date, part].astype(F32)], axis=0
+            in_order(*pair), axis=0
         ).astype(BF16)
-        copies[part].wait()
+        copies[2 + part].wait()
         for tile in range(NT + 1):
             first = max(tile * TILE - half, 0)
             last = min(tile * TILE + half, COLS)
@@ -108,71 +146,116 @@
                 if tile > 0:
                     at = (tile - 1) * 2 * ROWS + place
                     wide[at : at + ROWS, TILE : 2 * TILE] = piece
-    out[...] = dot(wide_hi[...], rg_hi) + (dot(wide_lo[...], rg_hi) + dot(wide_hi[...], rg_lo))
-
-
-def resample(date, scalars, slc, before, after):
+    at = 0
+    stacks = [near_out] + far_out
+    for stack in stacks:
+        count = stack.shape[0]
+        hi, lo = wide_hi[at : at + count], wide_lo[at : at + count]
+        stack[...] = dot(hi, rg_hi) + (dot(lo, rg_hi) + dot(hi, rg_lo))
+        at += count
+    power[...] = jnp.zeros(power.shape, F32)
+    box = column_box()
+    for tile in range(NT):
+        s0, s1 = both_parts(stacks, tile)
+        add_columns(power, box, tile, s0 * s0 + s1 * s1)
+
+
+def column_box():
+    reach = iota((32, TILE), 1) // LOOK_RG + 8 - iota((32, TILE), 0)
+    return jnp.where(jnp.abs(reach) <= RADIUS, 1.0, 0.0).astype(BF16)
+
+
+def both_parts(stacks, tile):
+    at = tile * 2 * ROWS
+    for stack in stacks:
+        if at < stack.shape[0]:
+            break
+        at -= stack.shape[0]
+    return stack[at : at + ROWS], stack[at + ROWS : at + 2 * ROWS]
+
+
+def add_columns(columns, box, tile, values):
+    high, low = two_halves(values)
+    nt = ((1,), (1,))
+    columns[tile * 16 : tile * 16 + 32] += dot(box, high, nt) + dot(box, low, nt)
+
+
+def resample(date, far, scalars, slc, partner, other):
+    spaces = (VMEM, pltpu.HBM) if far else (VMEM,)
+    rows = NT * 2 * ROWS // len(spaces)
     return pl.pallas_call(
         functools.partial(resample_kernel, date),
         compiler_params=GRANT,
-        out_shape=VMEM((NT * 2 * ROWS, TILE), F32),
+        out_shape=tuple(space((rows, TILE), F32) for space in spaces)
+        + (VMEM((LCOLS + 16, ROWS), F32),),
         in_specs=[pl.BlockSpec(memory_space=SMEM)] * 5
-        + [pl.BlockSpec(memory_space=pl.ANY)]
-        + [pl.BlockSpec(memory_space=VMEM)] * 2,
-        out_specs=pl.BlockSpec(memory_space=VMEM),
+        + [pl.BlockSpec(memory_space=pl.ANY)] * 3,
+        out_specs=(pl.BlockSpec(memory_space=VMEM),) * (len(spaces) + 1),
         scratch_shapes=[
             pltpu.VMEM((2, ROWS + 16, COLS), BF16),
+            pltpu.VMEM((2, 2, 8, COLS), BF16),
             pltpu.VMEM((NT * 2 * ROWS, 2 * TILE), BF16),
             pltpu.VMEM((NT * 2 * ROWS, 2 * TILE), BF16),
-            pltpu.SemaphoreType.DMA((2,)),
+            pltpu.SemaphoreType.DMA((4,)),
         ],
         cost_estimate=pl.CostEstimate(
             flops=3_000_000_000, transcendentals=0, bytes_accessed=1_600_000
         ),
-    )(*scalars, slc, *near(before, after))
-
-
-def looks_kernel(center, first, second, out, columns):
+    )(*scalars, *far_away(slc, partner, other))
+
+
+FAR = NT * ROWS
+
+
+def looks_kernel(center, near_first, second, power0, power1, far, out, columns, far_first, arrived):
+    copy = pltpu.make_async_copy(far, far_first, arrived)
+    copy.start()
+    box = column_box()
     columns[...] = jnp.zeros(columns.shape, F32)
-    reach = iota((32, TILE), 1) // LOOK_RG + 8 - iota((32, TILE), 0)
-    box = jnp.where(jnp.abs(reach) <= RADIUS, 1.0, 0.0).astype(BF16)
     for tile in range(NT):
+        if tile == NT // 2:
+            copy.wait()
         at = tile * TILE
         e0 = center[0:8, :, at : at + TILE].astype(F32).reshape(ROWS, TILE)
         e1 = center[8:16, :, at : at + TILE].astype(F32).reshape(ROWS, TILE)
-        cross = []
-        power = []
-        for stack in (first, second):
-            s0 = stack[tile * 2 * ROWS : tile * 2 * ROWS + ROWS]
-            s1 = stack[tile * 2 * ROWS + ROWS : (tile + 1) * 2 * ROWS]
-            cross.append(e0 * s0 + e1 * s1)
-            cross.append(e1 * s0 - e0 * s1)
-            power.append(s0 * s0 + s1 * s1)
-        power.append(e0 * e0 + e1 * e1)
-        high, low = two_halves(jnp.concatenate(cross + power, axis=0))
-        nt = ((1,), (1,))
-        columns[tile * 16 : tile * 16 + 32] += dot(box, high, nt) + dot(box, low, nt)
-    quantities = 7
-    pixel = iota((quantities * ROWS, 128), 0)
-    box_rows = jnp.where(pixel // LOOK_AZ == iota((quantities * ROWS, 128), 1), 1.0 / 64, 0.0)
-    box_rows = box_rows.astype(BF16)
-    high, low = two_halves(columns[8 : 8 + LCOLS])
-    out[...] = dot(high, box_rows) + dot(low, box_rows)
-
-
-def looks(center, first, second):
+        values = []
+        for stacks in ((near_first, far_first), (second,)):
+            s0, s1 = both_parts(stacks, tile)
+            values += [e0 * s0 + e1 * s1, e1 * s0 - e0 * s1]
+        values.append(e0 * e0 + e1 * e1)
+        add_columns(columns, box, tile, jnp.concatenate(values, axis=0))
+
+    total = jnp.zeros((LCOLS, 128), F32)
+    quantity = 0
+    for part in (columns, power0, power1):
+        shape = (part.shape[1], 128)
+        hit = iota(shape, 0) // LOOK_AZ == iota(shape, 1) - quantity * LOOKS
+        box_rows = jnp.where(hit, 1.0 / (LOOK_AZ * LOOK_RG), 0.0).astype(BF16)
+        high, low = two_halves(part[8 : 8 + LCOLS])
+        total = total + (dot(high, box_rows) + dot(low, box_rows))
+        quantity += part.shape[1] // ROWS
+    out[...] = total
+
+
+def looks(center, near_first, far_first, second, power0, power1):
     return pl.pallas_call(
         looks_kernel,
         name="looks",
         compiler_params=GRANT,
         out_shape=VMEM((LCOLS, 128), F32),
-        in_specs=[pl.BlockSpec(memory_space=VMEM)] * 3,
+        in_specs=[pl.BlockSpec(memory_space=VMEM)] * 5 + [pl.BlockSpec(memory_space=pl.ANY)],
         out_specs=pl.BlockSpec(memory_space=VMEM),
-        scratch_shapes=[pltpu.VMEM((LCOLS + 16, 7 * ROWS), F32)],
-    )(*near(center, first, second))
-
-
-def coherence_kernel(own, before, after, out, kept):
+        scratch_shapes=[
+            pltpu.VMEM((LCOLS + 16, 5 * ROWS), F32),
+            pltpu.VMEM((FAR, TILE), F32),
+            pltpu.SemaphoreType.DMA,
+        ],
+    )(
+        *near(center, near_first, second, power0, power1), *far_away(far_first)
+    )
+
+
+def coherence_kernel(own, partner, other, out, kept):
     source = iota((384, 384), 0)
     target = iota((384, 384), 1)
     row_in = source % 16 + (source // 128) * 16 - 16
@@ -182,12 +265,13 @@
     slot = target % 128
     date = slot // 32
     wanted = jnp.where(
-        group == 0, date * 2 + slot % 2, jnp.where(group == 1, 4 + date, 6)
+        group == 0, date * 2 + slot % 2, jnp.where(group == 1, 5 + date, 4)
     )
     reach = row_in - (slot % 32) // 2
     hit = (quantity == wanted) & (jnp.abs(reach) <= RADIUS) & (slot < 64)
     box = jnp.where(hit, 1.0, 0.0).astype(BF16)
-    high, low = two_halves(jnp.concatenate([before[...], own[...], after[...]], axis=1))
+    before, after = in_order(partner[...], other[...])
+    high, low = two_halves(jnp.concatenate([before, own[...], after], axis=1))
     summed = dot(high, box) + dot(low, box)
     cross = summed[:, 0:128]
     scale = 1.0 / jnp.sqrt(summed[:, 256:384] * summed[:, 128:256] + EPS)
@@ -198,7 +282,7 @@
     out[...] = jnp.stack([pair, pieces[2]], axis=1).astype(BF16)
 
 
-def coherence(own, before, after):
+def coherence(own, partner, other):
     return pl.pallas_call(
         coherence_kernel,
         name="coherence",
@@ -207,7 +291,7 @@
         in_specs=[pl.BlockSpec(memory_space=VMEM)] * 3,
         out_specs=pl.BlockSpec(memory_space=VMEM),
         scratch_shapes=[pltpu.VMEM((LCOLS, 128), F32)],
-    )(*near(own, before, after))
+    )(*near(own, partner, other))
 
 
 def finish_kernel(arrived, out, mean):
@@ -251,6 +335,57 @@
     )(*near(arrived))
 
 
+def quarters_kernel(slc, *rest):
+    *outs, arrived = rest
+    copies = []
+    for out, homes in zip(outs, HOMES):
+        for at, (x, y) in enumerate(homes):
+            part, block = divmod(x * 4 + y, 8)
+            source = slc.at[0, part, pl.ds(block * 8, 8)]
+            copies.append(pltpu.make_async_copy(source, out.at[at], arrived.at[len(copies)]))
+    for copy in copies:
+        copy.start()
+    for copy in copies:
+        copy.wait()
+
+
+def quarters_of(slc):
+    return pl.pallas_call(
+        quarters_kernel,
+        name="quarters",
+        compiler_params=GRANT,
+        out_shape=(VMEM((4, 8, COLS), BF16),) * 4,
+        in_specs=[pl.BlockSpec(memory_space=pl.ANY)],
+        out_specs=(pl.BlockSpec(memory_space=VMEM),) * 4,
+        scratch_shapes=[pltpu.SemaphoreType.DMA((16,))],
+    )(*far_away(slc))
+
+
+def copies_kernel(own, *rest):
+    *pieces, out, value, sent = rest
+    total = own[0]
+    for piece in pieces:
+        total = total + piece[0]
+    value[...] = total
+    copies = [pltpu.make_async_copy(value, out.at[at], sent.at[at]) for at in range(16)]
+    for copy in copies:
+        copy.start()
+    for copy in copies:
+        copy.wait()
+
+
+def copies_of(own, pieces):
+    return pl.pallas_call(
+        copies_kernel,
+        name="copies",
+        compiler_params=GRANT,
+        out_shape=pltpu.HBM((16, 8, COLS), BF16),
+        in_specs=[pl.BlockSpec(memory_space=VMEM)] * 4,
+        out_specs=pl.BlockSpec(memory_space=pl.ANY),
+        scratch_shapes=[pltpu.VMEM((8, COLS), BF16), pltpu.SemaphoreType.DMA((16,))],
+    )(*near(own, *pieces))
+
+
 def place(z, x, y):
     return z * 16 + x * 4 + y
 
@@ -264,21 +399,16 @@
 
 
 def body(slc, az_shift, rg_shift, az_frac, rg_frac):
-    up = [(i, i + 1) for i in range(3)]
-    down = [(i + 1, i) for i in range(3)]
     scalars = (az_shift, rg_shift, az_frac, rg_frac, jnp.asarray(kernel_bank()))
-    quarters = [
-        slc[0, part, 32 * half : 32 * half + 32].reshape(4, 8, COLS)
-        for part in range(2)
-        for half in range(2)
-    ]
-
-    first = lax.axis_index("date") == 0
+    quarters = quarters_of(slc)
+    kept = jnp.where(lax.axis_index("date") == 0, quarters[0], jnp.zeros_like(quarters[0]))
+    kept = lax.optimization_barrier(kept)
+
     pieces = [lax.ppermute(quarters[k], "date", [(0, place(0, *HOMES[k][0]))]) for k in range(1, 4)]
-    before = lax.ppermute(slc[:, :, ROWS - 8 :], "az", up)
-    after = lax.ppermute(slc[:, :, :8], "az", down)
-    pieces, before, after = lax.optimization_barrier((pieces, before, after))
-    quarter = jnp.where(first, quarters[0], jnp.zeros_like(quarters[0])) + sum(pieces)
+    head, tail = slc[:, :, :8], slc[:, :, ROWS - 8 :]
+    odd = odd_block()
+    edges = swapped(jnp.where(odd, head, tail), jnp.where(odd, tail, head))
+    quarter = kept + sum(pieces)
 
     pieces = [
         lax.ppermute(
@@ -288,24 +418,21 @@
         )
         for k in range(1, 4)
     ]
-    early = resample(0, scalars, slc, before, after)
-    pieces, early = lax.optimization_barrier((pieces, early))
     chunk = quarter[0:1] + sum(pieces)
 
     flat = [home for homes in HOMES for home in homes]
     pieces = [
         lax.ppermute(chunk, "date", [(place(0, *home), place(k, *home)) for home in flat])
-        for k in (2, 1, 3)
+        for k in (1, 3, 2)
     ]
-    late = resample(1, scalars, slc, before, after)
-    pieces, late = lax.optimization_barrier((pieces, late))
-    whole = chunk + sum(pieces)
-
-    planes = [[place(z, *home) for home in flat] for z in range(4)]
-    copies = jnp.broadcast_to(whole, (16,) + whole.shape[1:])
+
+    planes = [[place(z, x, y) for x in range(4) for y in range(4)] for z in range(4)]
+    copies = copies_of(chunk, pieces)
     center = lax.all_to_all(copies, "date", 0, 0, axis_index_groups=planes, tiled=True)
-    own = looks(center, early, late)
-    outgoing = coherence(own, lax.ppermute(own, "az", up), lax.ppermute(own, "az", down))
+    near_first, far_first, power0 = resample(0, True, scalars, slc, *edges)
+    second, power1 = resample(1, False, scalars, slc, *edges)
+    own = looks(center, near_first, far_first, second, power0, power1)
+    outgoing = coherence(own, *swapped(own, own))
     arrived = lax.all_to_all(outgoing, "date", split_axis=0, concat_axis=0, tiled=True)
     rows, mean = finish(arrived)
     return rows.reshape(3, LOOKS, 2, 128), mean

time: 83.8 us -> 76.4 us (0.912)
  blocking collectives: 36.3 us -> 16.5 us
  waiting for transfers between devices: 8.27 us -> 14.7 us
  Pallas kernels: 11.3 us -> 15.1 us
  starting transfers between devices: 23.3 us -> 25.9 us
  local copies, waits for them, and re-layouts: 3.1 us -> 1.39 us
  other arithmetic: 0.09 us -> 1.14 us
    all_to_all x1 -> x0, blocking collectives: 16.4 us -> none  [body(): lax.all_to_all(copies, 'date', 0, 0, axis_index_groups=planes, tiled=True)]
    all_to_all x0 -> x1, starting transfers between devices: none -> 7.36 us  [body(): lax.all_to_all(copies, 'date', 0, 0, axis_index_groups=planes, tiled=True)]
    all_to_all x0 -> x1, waiting for transfers between devices: none -> 4.97 us  [body(): lax.all_to_all(copies, 'date', 0, 0, axis_index_groups=planes, tiled=True)]
    ppermute x4, starting transfers between devices: 8.92 us -> 4.03 us  [the longest x2 3.84 us: swapped(): lax.ppermute(to_other, 'az', [(1, 2), (2, 1)])]
    all_to_all x1, blocking collectives: 19.9 us -> 16.5 us  [body(): lax.all_to_all(outgoing, 'date', split_axis=0, concat_axis=0, tiled=True)]
    pallas_call x0 -> x2, Pallas kernels: none -> 2.31 us  [the longest x1 1.27 us: quarters_of(): pl.pallas_call(quarters_kernel, name='quarters', compiler_params=GRANT, o...]
    slice x1 -> x0, local copies, waits for them, and re-layouts: 1.83 us -> none  [body(): after = lax.ppermute(slc[:, :, :8], 'az', down)]
    ppermute x3, waiting for transfers between devices: 0.01 us -> 1.72 us  [body(): lax.ppermute(quarter[k:k + 1], 'date', [(place(0, *homes[0]), place(0, *h...]
  transfers between devices with their start and end apart: 13 -> 14, of which waited for: 5 -> 7; matrix products, arithmetic and copies ran while one was open for 1% -> 1% of each run, Pallas kernels for 9% -> 13%
where the time goes in v1:
time: 76.4 us; the launch traced here: 75.8 us
  starting transfers between devices  25.9 us (34%)
  blocking collectives  16.5 us (22%)
  Pallas kernels  15.1 us (20%)
  waiting for transfers between devices  14.7 us (19%)
  local copies, waits for them, and re-layouts  1.39 us (2%)
  other arithmetic  1.14 us (1%)
  between operations  0.94 us (1%)
    all_to_all x1, blocking collectives, body(): lax.all_to_all(outgoing, 'date', split_axis=0, concat_axis=0, tiled=True)  16.5 us
    pallas_call x2, Pallas kernels, resample(): pl.pallas_call(functools.partial(resample_kernel, date), compiler_params=...  8.88 us
    all_to_all x1, starting transfers between devices, body(): lax.all_to_all(copies, 'date', 0, 0, axis_index_groups=planes, tiled=True)  7.36 us
    ppermute x3, starting transfers between devices, body(): lax.ppermute(quarters[k], 'date', [(0, place(0, *HOMES[k][0]))])  6.65 us
    all_to_all x1, waiting for transfers between devices, body(): lax.all_to_all(copies, 'date', 0, 0, axis_index_groups=planes, tiled=True)  4.97 us
    ppermute x3, waiting for transfers between devices, body(): lax.ppermute(quarters[k], 'date', [(0, place(0, *HOMES[k][0]))])  4.1 us
    ppermute x3, starting transfers between devices, body(): lax.ppermute(chunk, 'date', [(place(0, *home), place(k, *home)) for home...  4.01 us
    ppermute x2, waiting for transfers between devices, swapped(): lax.ppermute(to_other, 'az', [(1, 2), (2, 1)])  3.91 us
  transfers between devices with their start and end apart: 14, of which 7 were waited for; matrix products, arithmetic and copies ran while one was open for 1% of the time, Pallas kernels for 13%

profile of v1, /device:TPU:32, one launch (start us, length us, event | category | flops | bytes accessed | tf_op | source)
XLA Modules:
  0.0 75.8 jit_solution(7590361661622134832)
XLA Ops:
  0.6 1.3 %quarters.1 = (bf16[4,8,3072]{2,1,0:T(8,128)(2,1)S(1)}, bf16[4,8,3072]{2,1,0:T(8,128)(2,1)S(1)}, bf16[4,8,3072]{2,1,0:T(8,128)(2,1)S(1)}, bf16[4,8,3072]{2,1,0:T(8,128)(2,1)S(1)}) custom-call(bf16[2,2,64,3072]{3,2,1,0:T(8,128)(2,1)} %own.3), custom_call_target="tpu_custom_call" | custom-call | tf_op jit(solution)/shard_map/quarters/pallas_call | solution.py:353
  1.9 3.4 %collective-permute-start = (bf16[4,8,3072]{2,1,0:T(8,128)(2,1)S(1)}, bf16[4,8,3072]{2,1,0:T(8,128)(2,1)S(1)}, u32[]{:S(2)}, u32[]{:S(2)}) collective-permute-start(bf16[4,8,3072]{2,1,0:T(8,128)(2,1)S(1)} %get-tuple-element.14), channel_id=1, source_target_pairs={{0,16},{1,17},{2,18},{3,19}} | collective-permute-start | bytes 589832 | tf_op jit(solution)/shard_map/ppermute | solution.py:407
  5.3 1.9 %collective-permute-start.1 = (bf16[4,8,3072]{2,1,0:T(8,128)(2,1)S(1)}, bf16[4,8,3072]{2,1,0:T(8,128)(2,1)S(1)}, u32[]{:S(2)}, u32[]{:S(2)}) collective-permute-start(bf16[4,8,3072]{2,1,0:T(8,128)(2,1)S(1)} %get-tuple-element.15), channel_id=1, source_target_pairs={{0,48},{1,49},{2,50},{3,51}} | collective-permute-start | bytes 589832 | tf_op jit(solution)/shard_map/ppermute | solution.py:407
  7.3 1.3 %collective-permute-start.2 = (bf16[4,8,3072]{2,1,0:T(8,128)(2,1)S(1)}, bf16[4,8,3072]{2,1,0:T(8,128)(2,1)S(1)}, u32[]{:S(2)}, u32[]{:S(2)}) collective-permute-start(bf16[4,8,3072]{2,1,0:T(8,128)(2,1)S(1)} %get-tuple-element.16), channel_id=1, source_target_pairs={{0,4},{1,5},{2,6},{3,7}} | collective-permute-start | bytes 589832 | tf_op jit(solution)/shard_map/ppermute | solution.py:407
  9.4 1.9 %collective-permute-done.1 = bf16[4,8,3072]{2,1,0:T(8,128)(2,1)S(1)} collective-permute-done((bf16[4,8,3072]{2,1,0:T(8,128)(2,1)S(1)}, bf16[4,8,3072]{2,1,0:T(8,128)(2,1)S(1)}, u32[]{:S(2)}, u32[]{:S(2)}) %collective-permute-start.1) | collective-permute-done | bytes 196640 | tf_op jit(solution)/shard_map/ppermute | solution.py:407
  11.4 1.3 %collective-permute-done.2 = bf16[4,8,3072]{2,1,0:T(8,128)(2,1)S(1)} collective-permute-done((bf16[4,8,3072]{2,1,0:T(8,128)(2,1)S(1)}, bf16[4,8,3072]{2,1,0:T(8,128)(2,1)S(1)}, u32[]{:S(2)}, u32[]{:S(2)}) %collective-permute-start.2) | collective-permute-done | bytes 196640 | tf_op jit(solution)/shard_map/ppermute | solution.py:407
  12.8 1.3 %collective-permute-start.4 = (bf16[1,8,3072]{2,1,0:T(8,128)(2,1)S(1)}, bf16[1,8,3072]{2,1,0:T(8,128)(2,1)S(1)}, u32[]{:S(2)}, u32[]{:S(2)}) collective-permute-start(bf16[1,8,3072]{2,1,0:T(8,128)(2,1)S(1)} %get-tuple-element.26), channel_id=1, source_target_pairs={{0,28},{16,20},{48,56},{4,24},{1,29},{17,21},{49,57},{5,25},{2,30}... | collective-permute-start | bytes 147464 | tf_op jit(solution)/shard_map/ppermute | solution.py:414
  14.1 1.3 %collective-permute-start.5 = (bf16[1,8,3072]{2,1,0:T(8,128)(2,1)S(1)}, bf16[1,8,3072]{2,1,0:T(8,128)(2,1)S(1)}, u32[]{:S(2)}, u32[]{:S(2)}) collective-permute-start(bf16[1,8,3072]{2,1,0:T(8,128)(2,1)S(1)} %get-tuple-element.27), channel_id=1, source_target_pairs={{0,60},{16,36},{48,44},{4,40},{1,61},{17,37},{49,45},{5,41},{2,62}... | collective-permute-start | bytes 147464 | tf_op jit(solution)/shard_map/ppermute | solution.py:414
  15.4 1.3 %collective-permute-start.3 = (bf16[1,8,3072]{2,1,0:T(8,128)(2,1)S(1)}, bf16[1,8,3072]{2,1,0:T(8,128)(2,1)S(1)}, u32[]{:S(2)}, u32[]{:S(2)}) collective-permute-start(bf16[1,8,3072]{2,1,0:T(8,128)(2,1)S(1)} %get-tuple-element.28), channel_id=1, source_target_pairs={{0,12},{16,32},{48,52},{4,8},{1,13},{17,33},{49,53},{5,9},{2,14},{... | collective-permute-start | bytes 147464 | tf_op jit(solution)/shard_map/ppermute | solution.py:414
  17.1 1.3 %collective-permute-done.3 = bf16[1,8,3072]{2,1,0:T(8,128)(2,1)S(1)} collective-permute-done((bf16[1,8,3072]{2,1,0:T(8,128)(2,1)S(1)}, bf16[1,8,3072]{2,1,0:T(8,128)(2,1)S(1)}, u32[]{:S(2)}, u32[]{:S(2)}) %collective-permute-start.3) | collective-permute-done | bytes 49184 | tf_op jit(solution)/shard_map/ppermute | solution.py:414
  18.5 1.4 %collective-permute-start.8 = (bf16[1,8,3072]{2,1,0:T(8,128)(2,1)S(1)}, bf16[1,8,3072]{2,1,0:T(8,128)(2,1)S(1)}, u32[]{:S(2)}, u32[]{:S(2)}) collective-permute-start(bf16[1,8,3072]{2,1,0:T(8,128)(2,1)S(1)} %slice_add_fusion.own), channel_id=1, source_target_pairs={{0,128},{12,140},{28,156},{60,188},{16,144},{32,160},{20,148},{36,... | collective-permute-start | bytes 147464 | tf_op jit(solution)/shard_map/ppermute | solution.py:425
  19.9 1.3 %collective-permute-start.7 = (bf16[1,8,3072]{2,1,0:T(8,128)(2,1)S(1)}, bf16[1,8,3072]{2,1,0:T(8,128)(2,1)S(1)}, u32[]{:S(2)}, u32[]{:S(2)}) collective-permute-start(bf16[1,8,3072]{2,1,0:T(8,128)(2,1)S(1)} %slice_add_fusion.own), channel_id=1, source_target_pairs={{0,192},{12,204},{28,220},{60,252},{16,208},{32,224},{20,212},{36,... | collective-permute-start | bytes 147464 | tf_op jit(solution)/shard_map/ppermute | solution.py:425
  21.2 1.3 %collective-permute-start.6 = (bf16[1,8,3072]{2,1,0:T(8,128)(2,1)S(1)}, bf16[1,8,3072]{2,1,0:T(8,128)(2,1)S(1)}, u32[]{:S(2)}, u32[]{:S(2)}) collective-permute-start(bf16[1,8,3072]{2,1,0:T(8,128)(2,1)S(1)} %slice_add_fusion.own), channel_id=1, source_target_pairs={{0,64},{12,76},{28,92},{60,124},{16,80},{32,96},{20,84},{36,100},{... | collective-permute-start | bytes 147464 | tf_op jit(solution)/shard_map/ppermute | solution.py:425
  22.5 1.1 %broadcast_select_fusion = (bf16[2,2,8,3072]{3,2,1,0:T(8,128)(2,1)S(1)}, bf16[2,2,8,3072]{3,2,1,0:T(8,128)(2,1)S(1)}) fusion(pred[]{:T(512)S(6)} %eq.7, bf16[2,2,64,3072]{3,2,1,0:T(8,128)(2,1)} %own.3), kind=kLoop, calls=%fused_computation.1 | loop fusion | flops 196608 | bytes 786433 | tf_op jit(solution)/shard_map/jit(_where)/select_n | solution.py:410
  23.6 1.9 %collective-permute-start.10 = (bf16[2,2,8,3072]{3,2,1,0:T(8,128)(2,1)S(1)}, bf16[2,2,8,3072]{3,2,1,0:T(8,128)(2,1)S(1)}, u32[]{:S(2)}, u32[]{:S(2)}) collective-permute-start(bf16[2,2,8,3072]{3,2,1,0:T(8,128)(2,1)S(1)} %get-tuple-element.24), channel_id=1, source_target_pairs={{1,2},{2,1},{5,6},{6,5},{9,10},{10,9},{13,14},{14,13},{17,18},{18,... | collective-permute-start | bytes 589832 | tf_op jit(solution)/shard_map/ppermute | solution.py:79
  26.7 7.4 %all-to-all-start = ((bf16[16,8,3072]{2,1,0:T(8,128)(2,1)}), bf16[16,8,3072]{2,1,0:T(8,128)(2,1)S(1)}, u32[]{:S(2)}, u32[]{:S(2)}) async-start(bf16[16,8,3072]{2,1,0:T(8,128)(2,1)} %copies.1), calls=%async_computation | async-start | bytes 1572864 | tf_op jit(solution)/shard_map/all_to_all | solution.py:431
  35.5 4.7 %shard_map.77 = (f32[768,256]{1,0:T(8,128)S(1)}, f32[768,256]{1,0:T(8,128)}, f32[208,64]{1,0:T(8,128)S(1)}) custom-call(s32[2]{0:T(128)S(1)} %copy-done, s32[2]{0:T(128)S(1)} %copy-done.1, s32[2]{0:T(128)S(1)} %copy-done.2, s32[2]{0:T(128)S(1)} %copy-done.3, f32[16,8]{1,0:T(8,128)S(1)} %copy-done.4, bf16[2,2,64,3072]{3,2,1,0:T(8,128)(2,1)} %own.3, ...), custom_call_target="tpu_custom_call" | custom-call | flops 3000000000 | bytes 1600000 | tf_op jit(solution)/shard_map/pallas_call | solution.py:186
  40.2 4.2 %shard_map.78 = (f32[1536,256]{1,0:T(8,128)S(1)}, f32[208,64]{1,0:T(8,128)S(1)}) custom-call(s32[2]{0:T(128)S(1)} %copy-done, s32[2]{0:T(128)S(1)} %copy-done.1, s32[2]{0:T(128)S(1)} %copy-done.2, s32[2]{0:T(128)S(1)} %copy-done.3, f32[16,8]{1,0:T(8,128)S(1)} %copy-done.4, bf16[2,2,64,3072]{3,2,1,0:T(8,128)(2,1)} %own.3, bf16[2,2,8,3072]{3,2,1,0:T(8,128)(2,1)} %copy-done.6, ...), custom_call_target="tpu_custom_call" | custom-call | flops 3000000000 | bytes 1600000 | tf_op jit(solution)/shard_map/pallas_call | solution.py:186
  44.3 5.0 %all-to-all-done.center = bf16[16,8,3072]{2,1,0:T(8,128)(2,1)S(1)} async-done(((bf16[16,8,3072]{2,1,0:T(8,128)(2,1)}), bf16[16,8,3072]{2,1,0:T(8,128)(2,1)S(1)}, u32[]{:S(2)}, u32[]{:S(2)}) %all-to-all-start) | async-done | bytes 786464 | tf_op jit(solution)/shard_map/all_to_all | solution.py:431
  49.3 2.1 %looks.1.own = f32[192,128]{1,0:T(8,128)S(1)} custom-call(bf16[16,8,3072]{2,1,0:T(8,128)(2,1)S(1)} %all-to-all-done.center, f32[768,256]{1,0:T(8,128)S(1)} %get-tuple-element.17.near_first, f32[1536,256]{1,0:T(8,128)S(1)} %get-tuple-element.18.second, f32[208,64]{1,0:T(8,128)S(1)} %get-tuple-element.19.power0, f32[208,64]{1,0:T(8,128)S(1)} %get-tuple-element.20.power1, ...), custom_call_target="tpu_custom_call" | custom-call | tf_op jit(solution)/shard_map/looks/pallas_call | solution.py:241
  51.4 1.9 %collective-permute-start.12 = (f32[192,128]{1,0:T(8,128)S(1)}, f32[192,128]{1,0:T(8,128)S(1)}, u32[]{:S(2)}, u32[]{:S(2)}) collective-permute-start(f32[192,128]{1,0:T(8,128)S(1)} %looks.1.own), channel_id=1, source_target_pairs={{1,2},{2,1},{5,6},{6,5},{9,10},{10,9},{13,14},{14,13},{17,18},{18,... | collective-permute-start | bytes 294920 | tf_op jit(solution)/shard_map/ppermute | solution.py:79
  53.4 3.9 %collective-permute-done.12.other = f32[192,128]{1,0:T(8,128)S(1)} collective-permute-done((f32[192,128]{1,0:T(8,128)S(1)}, f32[192,128]{1,0:T(8,128)S(1)}, u32[]{:S(2)}, u32[]{:S(2)}) %collective-permute-start.12) | collective-permute-done | bytes 98336 | tf_op jit(solution)/shard_map/ppermute | solution.py:79
  57.9 16.5 %all_to_all.10.arrived = bf16[64,2,128]{2,1,0:T(2,128)(2,1)S(1)} all-to-all(bf16[64,2,128]{2,1,0:T(2,128)(2,1)S(1)} %coherence.1), channel_id=1, replica_groups=mesh['date'=64,'az'=4] {'date'}, dimensions={0} | all-to-all | bytes 65536 | tf_op jit(solution)/shard_map/all_to_all | solution.py:436
  74.5 1.3 %finish.1 = (bf16[96,128]{1,0:T(8,128)(2,1)}, f32[3,16]{1,0:T(4,128)}) custom-call(bf16[64,2,128]{2,1,0:T(2,128)(2,1)S(1)} %all_to_all.10.arrived), custom_call_target="tpu_custom_call" | custom-call | tf_op jit(solution)/shard_map/finish/pallas_call | solution.py:325
  (31 shorter events, 4.6 us)
Async XLA Ops:
  1.9 7.5 %collective-permute-start = (bf16[4,8,3072]{2,1,0:T(8,128)(2,1)S(1)}, bf16[4,8,3072]{2,1,0:T(8,128)(2,1)S(1)}, u32[]{:S(2)}, u32[]{:S(2)}) collective-permute-start(bf16[4,8,3072]{2,1,0:T(8,128)(2,1)S(1)} %get-tuple-element.14), channel_id=1, source_target_pairs={{0,16},{1,17},{2,18},{3,19}} | collective-permute-start | bytes 589832 | tf_op jit(solution)/shard_map/ppermute | solution.py:407
  5.3 6.1 %collective-permute-start.1 = (bf16[4,8,3072]{2,1,0:T(8,128)(2,1)S(1)}, bf16[4,8,3072]{2,1,0:T(8,128)(2,1)S(1)}, u32[]{:S(2)}, u32[]{:S(2)}) collective-permute-start(bf16[4,8,3072]{2,1,0:T(8,128)(2,1)S(1)} %get-tuple-element.15), channel_id=1, source_target_pairs={{0,48},{1,49},{2,50},{3,51}} | collective-permute-start | bytes 589832 | tf_op jit(solution)/shard_map/ppermute | solution.py:407
  7.3 5.4 %collective-permute-start.2 = (bf16[4,8,3072]{2,1,0:T(8,128)(2,1)S(1)}, bf16[4,8,3072]{2,1,0:T(8,128)(2,1)S(1)}, u32[]{:S(2)}, u32[]{:S(2)}) collective-permute-start(bf16[4,8,3072]{2,1,0:T(8,128)(2,1)S(1)} %get-tuple-element.16), channel_id=1, source_target_pairs={{0,4},{1,5},{2,6},{3,7}} | collective-permute-start | bytes 589832 | tf_op jit(solution)/shard_map/ppermute | solution.py:407
  12.8 3.9 %collective-permute-start.4 = (bf16[1,8,3072]{2,1,0:T(8,128)(2,1)S(1)}, bf16[1,8,3072]{2,1,0:T(8,128)(2,1)S(1)}, u32[]{:S(2)}, u32[]{:S(2)}) collective-permute-start(bf16[1,8,3072]{2,1,0:T(8,128)(2,1)S(1)} %get-tuple-element.26), channel_id=1, source_target_pairs={{0,28},{16,20},{48,56},{4,24},{1,29},{17,21},{49,57},{5,25},{2,30}... | collective-permute-start | bytes 147464 | tf_op jit(solution)/shard_map/ppermute | solution.py:414
  14.1 3.0 %collective-permute-start.5 = (bf16[1,8,3072]{2,1,0:T(8,128)(2,1)S(1)}, bf16[1,8,3072]{2,1,0:T(8,128)(2,1)S(1)}, u32[]{:S(2)}, u32[]{:S(2)}) collective-permute-start(bf16[1,8,3072]{2,1,0:T(8,128)(2,1)S(1)} %get-tuple-element.27), channel_id=1, source_target_pairs={{0,60},{16,36},{48,44},{4,40},{1,61},{17,37},{49,45},{5,41},{2,62}... | collective-permute-start | bytes 147464 | tf_op jit(solution)/shard_map/ppermute | solution.py:414
  15.4 3.0 %collective-permute-start.3 = (bf16[1,8,3072]{2,1,0:T(8,128)(2,1)S(1)}, bf16[1,8,3072]{2,1,0:T(8,128)(2,1)S(1)}, u32[]{:S(2)}, u32[]{:S(2)}) collective-permute-start(bf16[1,8,3072]{2,1,0:T(8,128)(2,1)S(1)} %get-tuple-element.28), channel_id=1, source_target_pairs={{0,12},{16,32},{48,52},{4,8},{1,13},{17,33},{49,53},{5,9},{2,14},{... | collective-permute-start | bytes 147464 | tf_op jit(solution)/shard_map/ppermute | solution.py:414
  18.4 17.0 %copy-start = (s32[2]{0:T(128)S(1)}, s32[2]{0:T(128)}, u32[]{:S(2)}) copy-start(s32[2]{0:T(128)} %azs.3) | copy-start | bytes 28
  18.4 17.0 %copy-start.1 = (s32[2]{0:T(128)S(1)}, s32[2]{0:T(128)}, u32[]{:S(2)}) copy-start(s32[2]{0:T(128)} %rgs.3) | copy-start | bytes 28
  18.4 17.0 %copy-start.2 = (s32[2]{0:T(128)S(1)}, s32[2]{0:T(128)}, u32[]{:S(2)}) copy-start(s32[2]{0:T(128)} %azf.3) | copy-start | bytes 28
  18.5 17.0 %copy-start.3 = (s32[2]{0:T(128)S(1)}, s32[2]{0:T(128)}, u32[]{:S(2)}) copy-start(s32[2]{0:T(128)} %rgf.3) | copy-start | bytes 28
  18.5 17.0 %copy-start.4 = (f32[16,8]{1,0:T(8,128)S(1)}, f32[16,8]{1,0:T(8,128)}, u32[]{:S(2)}) copy-start(f32[16,8]{1,0:T(8,128)} %constant.20.clone.bank) | copy-start | bytes 1540
  18.5 7.1 %collective-permute-start.8 = (bf16[1,8,3072]{2,1,0:T(8,128)(2,1)S(1)}, bf16[1,8,3072]{2,1,0:T(8,128)(2,1)S(1)}, u32[]{:S(2)}, u32[]{:S(2)}) collective-permute-start(bf16[1,8,3072]{2,1,0:T(8,128)(2,1)S(1)} %slice_add_fusion.own), channel_id=1, source_target_pairs={{0,128},{12,140},{28,156},{60,188},{16,144},{32,160},{20,148},{36,... | collective-permute-start | bytes 147464 | tf_op jit(solution)/shard_map/ppermute | solution.py:425
  19.9 5.7 %collective-permute-start.7 = (bf16[1,8,3072]{2,1,0:T(8,128)(2,1)S(1)}, bf16[1,8,3072]{2,1,0:T(8,128)(2,1)S(1)}, u32[]{:S(2)}, u32[]{:S(2)}) collective-permute-start(bf16[1,8,3072]{2,1,0:T(8,128)(2,1)S(1)} %slice_add_fusion.own), channel_id=1, source_target_pairs={{0,192},{12,204},{28,220},{60,252},{16,208},{32,224},{20,212},{36,... | collective-permute-start | bytes 147464 | tf_op jit(solution)/shard_map/ppermute | solution.py:425
  21.2 4.4 %collective-permute-start.6 = (bf16[1,8,3072]{2,1,0:T(8,128)(2,1)S(1)}, bf16[1,8,3072]{2,1,0:T(8,128)(2,1)S(1)}, u32[]{:S(2)}, u32[]{:S(2)}) collective-permute-start(bf16[1,8,3072]{2,1,0:T(8,128)(2,1)S(1)} %slice_add_fusion.own), channel_id=1, source_target_pairs={{0,64},{12,76},{28,92},{60,124},{16,80},{32,96},{20,84},{36,100},{... | collective-permute-start | bytes 147464 | tf_op jit(solution)/shard_map/ppermute | solution.py:425
  23.6 10.5 %collective-permute-start.10 = (bf16[2,2,8,3072]{3,2,1,0:T(8,128)(2,1)S(1)}, bf16[2,2,8,3072]{3,2,1,0:T(8,128)(2,1)S(1)}, u32[]{:S(2)}, u32[]{:S(2)}) collective-permute-start(bf16[2,2,8,3072]{3,2,1,0:T(8,128)(2,1)S(1)} %get-tuple-element.24), channel_id=1, source_target_pairs={{1,2},{2,1},{5,6},{6,5},{9,10},{10,9},{13,14},{14,13},{17,18},{18,... | collective-permute-start | bytes 589832 | tf_op jit(solution)/shard_map/ppermute | solution.py:79
  25.5 8.6 %collective-permute-start.9 = (bf16[2,2,8,3072]{3,2,1,0:T(8,128)(2,1)S(1)}, bf16[2,2,8,3072]{3,2,1,0:T(8,128)(2,1)S(1)}, u32[]{:S(2)}, u32[]{:S(2)}) collective-permute-start(bf16[2,2,8,3072]{3,2,1,0:T(8,128)(2,1)S(1)} %get-tuple-element.25), channel_id=1, source_target_pairs={{0,1},{1,0},{2,3},{3,2},{4,5},{5,4},{6,7},{7,6},{8,9},{9,8},{10,11... | collective-permute-start | bytes 589832 | tf_op jit(solution)/shard_map/ppermute | solution.py:78
  26.7 22.6 %all-to-all-start = ((bf16[16,8,3072]{2,1,0:T(8,128)(2,1)}), bf16[16,8,3072]{2,1,0:T(8,128)(2,1)S(1)}, u32[]{:S(2)}, u32[]{:S(2)}) async-start(bf16[16,8,3072]{2,1,0:T(8,128)(2,1)} %copies.1), calls=%async_computation | async-start | bytes 1572864 | tf_op jit(solution)/shard_map/all_to_all | solution.py:431
  34.1 0.7 copy-start.5
  34.7 0.7 copy-start.6
  51.4 5.9 %collective-permute-start.12 = (f32[192,128]{1,0:T(8,128)S(1)}, f32[192,128]{1,0:T(8,128)S(1)}, u32[]{:S(2)}, u32[]{:S(2)}) collective-permute-start(f32[192,128]{1,0:T(8,128)S(1)} %looks.1.own), channel_id=1, source_target_pairs={{1,2},{2,1},{5,6},{6,5},{9,10},{10,9},{13,14},{14,13},{17,18},{18,... | collective-permute-start | bytes 294920 | tf_op jit(solution)/shard_map/ppermute | solution.py:79
  53.3 4.0 %collective-permute-start.11 = (f32[192,128]{1,0:T(8,128)S(1)}, f32[192,128]{1,0:T(8,128)S(1)}, u32[]{:S(2)}, u32[]{:S(2)}) collective-permute-start(f32[192,128]{1,0:T(8,128)S(1)} %looks.1.own), channel_id=1, source_target_pairs={{0,1},{1,0},{2,3},{3,2},{4,5},{5,4},{6,7},{7,6},{8,9},{9,8},{10,11... | collective-permute-start | bytes 294920 | tf_op jit(solution)/shard_map/ppermute | solution.py:78

commit v2 on v1

--- a/solution.py
+++ b/solution.py
@@ -82,18 +82,19 @@
 
 def resample_kernel(
     date,
-    azs,
-    rgs,
-    azf,
-    rgf,
-    bank,
-    own,
-    partner,
-    other,
-    near_out,
-    *rest,
+    count,
+    *refs,
 ):
-    *far_out, power, rows_in, edges, wide_hi, wide_lo, arrived = rest
+    tables, (own, partner, other), rest = refs[:5], refs[5:8], refs[8:]
+    stacks, power = rest[:count], rest[count]
+    rows_in, edges, wide_hi, wide_lo, arrived, *local = rest[count + 1 :]
+    loads = [
+        pltpu.make_async_copy(table, here, arrived.at[4 + at])
+        for at, (table, here) in enumerate(zip(tables, local))
+    ]
+    for load in loads:
+        load.start()
+    azs, rgs, azf, rgf, bank = local
     copies = [
         pltpu.make_async_copy(source.at[date], edges.at[at], arrived.at[2 + at])
         for at, source in enumerate((partner, other))
@@ -103,6 +104,8 @@
     ]
     for copy in copies:
         copy.start()
+    for load in loads:
+        load.wait()
     source = iota((ROWS, ROWS + 16), 1)
     source = jnp.where(
         source < ROWS, source, jnp.where(source < ROWS + 8, source - ROWS - 8, source - 8)
@@ -147,12 +150,11 @@
                     at = (tile - 1) * 2 * ROWS + place
                     wide[at : at + ROWS, TILE : 2 * TILE] = piece
     at = 0
-    stacks = [near_out] + far_out
     for stack in stacks:
-        count = stack.shape[0]
-        hi, lo = wide_hi[at : at + count], wide_lo[at : at + count]
+        size = stack.shape[0]
+        hi, lo = wide_hi[at : at + size], wide_lo[at : at + size]
         stack[...] = dot(hi, rg_hi) + (dot(lo, rg_hi) + dot(hi, rg_lo))
-        at += count
+        at += size
     power[...] = jnp.zeros(power.shape, F32)
     box = column_box()
     for tile in range(NT):
@@ -184,24 +186,25 @@
     spaces = (VMEM, pltpu.HBM) if far else (VMEM,)
     rows = NT * 2 * ROWS // len(spaces)
     return pl.pallas_call(
-        functools.partial(resample_kernel, date),
+        functools.partial(resample_kernel, date, len(spaces)),
         compiler_params=GRANT,
         out_shape=tuple(space((rows, TILE), F32) for space in spaces)
         + (VMEM((LCOLS + 16, ROWS), F32),),
-        in_specs=[pl.BlockSpec(memory_space=SMEM)] * 5
-        + [pl.BlockSpec(memory_space=pl.ANY)] * 3,
+        in_specs=[pl.BlockSpec(memory_space=pl.ANY)] * 8,
         out_specs=(pl.BlockSpec(memory_space=VMEM),) * (len(spaces) + 1),
         scratch_shapes=[
             pltpu.VMEM((2, ROWS + 16, COLS), BF16),
             pltpu.VMEM((2, 2, 8, COLS), BF16),
             pltpu.VMEM((NT * 2 * ROWS, 2 * TILE), BF16),
             pltpu.VMEM((NT * 2 * ROWS, 2 * TILE), BF16),
-            pltpu.SemaphoreType.DMA((4,)),
-        ],
+            pltpu.SemaphoreType.DMA((9,)),
+        ]
+        + [SMEM((2,), jnp.int32)] * 4
+        + [SMEM((KBANK, TAPS), F32)],
         cost_estimate=pl.CostEstimate(
             flops=3_000_000_000, transcendentals=0, bytes_accessed=1_600_000
         ),
-    )(*scalars, *far_away(slc, partner, other))
+    )(*far_away(*scalars, slc), partner, other)
 
 
 FAR = NT * ROWS
@@ -425,11 +428,13 @@
         lax.ppermute(chunk, "date", [(place(0, *home), place(k, *home)) for home in flat])
         for k in (1, 3, 2)
     ]
+    first = resample(0, True, scalars, slc, *edges)
+    pieces, first = lax.optimization_barrier((pieces, first))
 
     planes = [[place(z, x, y) for x in range(4) for y in range(4)] for z in range(4)]
     copies = copies_of(chunk, pieces)
     center = lax.all_to_all(copies, "date", 0, 0, axis_index_groups=planes, tiled=True)
-    near_first, far_first, power0 = resample(0, True, scalars, slc, *edges)
+    near_first, far_first, power0 = first
     second, power1 = resample(1, False, scalars, slc, *edges)
     own = looks(center, near_first, far_first, second, power0, power1)
     outgoing = coherence(own, *swapped(own, own))

time: 76.4 us -> 76.5 us (level)
  the two profiles are of different devices: /device:TPU:32 before, /device:TPU:1 now
where the time goes in v2:
time: 76.5 us; the launch traced here: 75.9 us
  starting transfers between devices  28.1 us (37%)
  blocking collectives  16.4 us (21%)
  Pallas kernels  14.8 us (19%)
  waiting for transfers between devices  13.5 us (18%)
  other arithmetic  1.13 us (1%)
  local copies, waits for them, and re-layouts  0.94 us (1%)
  between operations  0.92 us (1%)
    all_to_all x1, blocking collectives, body(): lax.all_to_all(outgoing, 'date', split_axis=0, concat_axis=0, tiled=True)  16.4 us
    ppermute x2, starting transfers between devices, swapped(): lax.ppermute(to_other, 'az', [(1, 2), (2, 1)])  9.32 us
    pallas_call x2, Pallas kernels, resample(): pl.pallas_call(functools.partial(resample_kernel, date, len(spaces)), com...  8.52 us
    all_to_all x1, waiting for transfers between devices, body(): lax.all_to_all(copies, 'date', 0, 0, axis_index_groups=planes, tiled=True)  7.81 us
    ppermute x3, starting transfers between devices, body(): lax.ppermute(quarters[k], 'date', [(0, place(0, *HOMES[k][0]))])  7.19 us
    ppermute x3, starting transfers between devices, body(): lax.ppermute(quarter[k:k + 1], 'date', [(place(0, *homes[0]), place(0, *h...  3.88 us
    ppermute x3, starting transfers between devices, body(): lax.ppermute(chunk, 'date', [(place(0, *home), place(k, *home)) for home...  3.88 us
    all_to_all x1, starting transfers between devices, body(): lax.all_to_all(copies, 'date', 0, 0, axis_index_groups=planes, tiled=True)  3.62 us
  transfers between devices with their start and end apart: 14, of which 5 were waited for; matrix products, arithmetic and copies ran while one was open for 1% of the time, Pallas kernels for 11%

profile of v2, /device:TPU:1, one launch (start us, length us, event | category | flops | bytes accessed | tf_op | source)
XLA Modules:
  0.0 75.9 jit_solution(11118618050929627947)
XLA Ops:
  0.6 1.3 %quarters.1 = (bf16[4,8,3072]{2,1,0:T(8,128)(2,1)S(1)}, bf16[4,8,3072]{2,1,0:T(8,128)(2,1)S(1)}, bf16[4,8,3072]{2,1,0:T(8,128)(2,1)S(1)}, bf16[4,8,3072]{2,1,0:T(8,128)(2,1)S(1)}) custom-call(bf16[2,2,64,3072]{3,2,1,0:T(8,128)(2,1)} %refs_5_.3), custom_call_target="tpu_custom_call" | custom-call | tf_op jit(solution)/shard_map/quarters/pallas_call | solution.py:356
  1.9 3.9 %collective-permute-start = (bf16[4,8,3072]{2,1,0:T(8,128)(2,1)S(1)}, bf16[4,8,3072]{2,1,0:T(8,128)(2,1)S(1)}, u32[]{:S(2)}, u32[]{:S(2)}) collective-permute-start(bf16[4,8,3072]{2,1,0:T(8,128)(2,1)S(1)} %get-tuple-element.20), channel_id=1, source_target_pairs={{0,16},{1,17},{2,18},{3,19}} | collective-permute-start | bytes 589832 | tf_op jit(solution)/shard_map/ppermute | solution.py:410
  5.9 1.9 %collective-permute-start.1 = (bf16[4,8,3072]{2,1,0:T(8,128)(2,1)S(1)}, bf16[4,8,3072]{2,1,0:T(8,128)(2,1)S(1)}, u32[]{:S(2)}, u32[]{:S(2)}) collective-permute-start(bf16[4,8,3072]{2,1,0:T(8,128)(2,1)S(1)} %get-tuple-element.21), channel_id=1, source_target_pairs={{0,48},{1,49},{2,50},{3,51}} | collective-permute-start | bytes 589832 | tf_op jit(solution)/shard_map/ppermute | solution.py:410
  7.8 1.3 %collective-permute-start.2 = (bf16[4,8,3072]{2,1,0:T(8,128)(2,1)S(1)}, bf16[4,8,3072]{2,1,0:T(8,128)(2,1)S(1)}, u32[]{:S(2)}, u32[]{:S(2)}) collective-permute-start(bf16[4,8,3072]{2,1,0:T(8,128)(2,1)S(1)} %get-tuple-element.22), channel_id=1, source_target_pairs={{0,4},{1,5},{2,6},{3,7}} | collective-permute-start | bytes 589832 | tf_op jit(solution)/shard_map/ppermute | solution.py:410
  9.4 1.9 %collective-permute-done.1 = bf16[4,8,3072]{2,1,0:T(8,128)(2,1)S(1)} collective-permute-done((bf16[4,8,3072]{2,1,0:T(8,128)(2,1)S(1)}, bf16[4,8,3072]{2,1,0:T(8,128)(2,1)S(1)}, u32[]{:S(2)}, u32[]{:S(2)}) %collective-permute-start.1) | collective-permute-done | bytes 196640 | tf_op jit(solution)/shard_map/ppermute | solution.py:410
  11.4 1.3 %collective-permute-done.2 = bf16[4,8,3072]{2,1,0:T(8,128)(2,1)S(1)} collective-permute-done((bf16[4,8,3072]{2,1,0:T(8,128)(2,1)S(1)}, bf16[4,8,3072]{2,1,0:T(8,128)(2,1)S(1)}, u32[]{:S(2)}, u32[]{:S(2)}) %collective-permute-start.2) | collective-permute-done | bytes 196640 | tf_op jit(solution)/shard_map/ppermute | solution.py:410
  12.7 1.3 %collective-permute-start.4 = (bf16[1,8,3072]{2,1,0:T(8,128)(2,1)S(1)}, bf16[1,8,3072]{2,1,0:T(8,128)(2,1)S(1)}, u32[]{:S(2)}, u32[]{:S(2)}) collective-permute-start(bf16[1,8,3072]{2,1,0:T(8,128)(2,1)S(1)} %get-tuple-element.38), channel_id=1, source_target_pairs={{0,28},{16,20},{48,56},{4,24},{1,29},{17,21},{49,57},{5,25},{2,30}... | collective-permute-start | bytes 147464 | tf_op jit(solution)/shard_map/ppermute | solution.py:417
  14.0 1.3 %collective-permute-start.5 = (bf16[1,8,3072]{2,1,0:T(8,128)(2,1)S(1)}, bf16[1,8,3072]{2,1,0:T(8,128)(2,1)S(1)}, u32[]{:S(2)}, u32[]{:S(2)}) collective-permute-start(bf16[1,8,3072]{2,1,0:T(8,128)(2,1)S(1)} %get-tuple-element.39), channel_id=1, source_target_pairs={{0,60},{16,36},{48,44},{4,40},{1,61},{17,37},{49,45},{5,41},{2,62}... | collective-permute-start | bytes 147464 | tf_op jit(solution)/shard_map/ppermute | solution.py:417
  15.3 1.3 %collective-permute-start.3 = (bf16[1,8,3072]{2,1,0:T(8,128)(2,1)S(1)}, bf16[1,8,3072]{2,1,0:T(8,128)(2,1)S(1)}, u32[]{:S(2)}, u32[]{:S(2)}) collective-permute-start(bf16[1,8,3072]{2,1,0:T(8,128)(2,1)S(1)} %get-tuple-element.40), channel_id=1, source_target_pairs={{0,12},{16,32},{48,52},{4,8},{1,13},{17,33},{49,53},{5,9},{2,14},{... | collective-permute-start | bytes 147464 | tf_op jit(solution)/shard_map/ppermute | solution.py:417
  16.6 1.1 %broadcast_select_fusion = (bf16[2,2,8,3072]{3,2,1,0:T(8,128)(2,1)S(1)}, bf16[2,2,8,3072]{3,2,1,0:T(8,128)(2,1)S(1)}) fusion(pred[]{:T(512)S(6)} %eq.7, bf16[2,2,64,3072]{3,2,1,0:T(8,128)(2,1)} %refs_5_.3), kind=kLoop, calls=%fused_computation.1 | loop fusion | flops 196608 | bytes 786433 | tf_op jit(solution)/shard_map/jit(_where)/select_n | solution.py:413
  17.7 5.0 %collective-permute-start.10 = (bf16[2,2,8,3072]{3,2,1,0:T(8,128)(2,1)S(1)}, bf16[2,2,8,3072]{3,2,1,0:T(8,128)(2,1)S(1)}, u32[]{:S(2)}, u32[]{:S(2)}) collective-permute-start(bf16[2,2,8,3072]{3,2,1,0:T(8,128)(2,1)S(1)} %get-tuple-element.36), channel_id=1, source_target_pairs={{1,2},{2,1},{5,6},{6,5},{9,10},{10,9},{13,14},{14,13},{17,18},{18,... | collective-permute-start | bytes 589832 | tf_op jit(solution)/shard_map/ppermute | solution.py:79
  22.8 1.3 %collective-permute-start.8 = (bf16[1,8,3072]{2,1,0:T(8,128)(2,1)S(1)}, bf16[1,8,3072]{2,1,0:T(8,128)(2,1)S(1)}, u32[]{:S(2)}, u32[]{:S(2)}) collective-permute-start(bf16[1,8,3072]{2,1,0:T(8,128)(2,1)S(1)} %slice_add_fusion.own), channel_id=1, source_target_pairs={{0,128},{12,140},{28,156},{60,188},{16,144},{32,160},{20,148},{36,... | collective-permute-start | bytes 147464 | tf_op jit(solution)/shard_map/ppermute | solution.py:428
  24.1 1.3 %collective-permute-start.7 = (bf16[1,8,3072]{2,1,0:T(8,128)(2,1)S(1)}, bf16[1,8,3072]{2,1,0:T(8,128)(2,1)S(1)}, u32[]{:S(2)}, u32[]{:S(2)}) collective-permute-start(bf16[1,8,3072]{2,1,0:T(8,128)(2,1)S(1)} %slice_add_fusion.own), channel_id=1, source_target_pairs={{0,192},{12,204},{28,220},{60,252},{16,208},{32,224},{20,212},{36,... | collective-permute-start | bytes 147464 | tf_op jit(solution)/shard_map/ppermute | solution.py:428
  25.4 1.3 %collective-permute-start.6 = (bf16[1,8,3072]{2,1,0:T(8,128)(2,1)S(1)}, bf16[1,8,3072]{2,1,0:T(8,128)(2,1)S(1)}, u32[]{:S(2)}, u32[]{:S(2)}) collective-permute-start(bf16[1,8,3072]{2,1,0:T(8,128)(2,1)S(1)} %slice_add_fusion.own), channel_id=1, source_target_pairs={{0,64},{12,76},{28,92},{60,124},{16,80},{32,96},{20,84},{36,100},{... | collective-permute-start | bytes 147464 | tf_op jit(solution)/shard_map/ppermute | solution.py:428
  26.7 4.5 %shard_map.77 = (f32[768,256]{1,0:T(8,128)S(1)}, f32[768,256]{1,0:T(8,128)}, f32[208,64]{1,0:T(8,128)S(1)}) custom-call(s32[2]{0:T(128)} %refs_0_.3, s32[2]{0:T(128)} %refs_1_.3, s32[2]{0:T(128)} %refs_2_.3, s32[2]{0:T(128)} %refs_3_.3, f32[16,8]{1,0:T(8,128)} %constant.20.clone.refs_4_, bf16[2,2,64,3072]{3,2,1,0:T(8,128)(2,1)} %refs_5_.3, ...), custom_call_target="tpu_custom_call" | custom-call | flops 3000000000 | bytes 1600000 | tf_op jit(solution)/shard_map/pallas_call | solution.py:188
  31.3 1.1 %copies.1 = bf16[16,8,3072]{2,1,0:T(8,128)(2,1)} custom-call(bf16[1,8,3072]{2,1,0:T(8,128)(2,1)S(1)} %slice_add_fusion.own, bf16[1,8,3072]{2,1,0:T(8,128)(2,1)S(1)} %collective-permute-done.6.rest_0_, bf16[1,8,3072]{2,1,0:T(8,128)(2,1)S(1)} %collective-permute-done.7.rest_1_, bf16[1,8,3072]{2,1,0:T(8,128)(2,1)S(1)} %collective-permute-done.8.rest_2_), custom_call_target="tpu_custom_call" | custom-call | tf_op jit(solution)/shard_map/copies/pallas_call | solution.py:381
  32.4 3.6 %all-to-all-start = ((bf16[16,8,3072]{2,1,0:T(8,128)(2,1)}), bf16[16,8,3072]{2,1,0:T(8,128)(2,1)S(1)}, u32[]{:S(2)}, u32[]{:S(2)}) async-start(bf16[16,8,3072]{2,1,0:T(8,128)(2,1)} %copies.1), calls=%async_computation | async-start | bytes 1572864 | tf_op jit(solution)/shard_map/all_to_all | solution.py:436
  37.0 4.0 %shard_map.78 = (f32[1536,256]{1,0:T(8,128)S(1)}, f32[208,64]{1,0:T(8,128)S(1)}) custom-call(s32[2]{0:T(128)} %refs_0_.3, s32[2]{0:T(128)} %refs_1_.3, s32[2]{0:T(128)} %refs_2_.3, s32[2]{0:T(128)} %refs_3_.3, f32[16,8]{1,0:T(8,128)} %constant.20.clone.refs_4_, bf16[2,2,64,3072]{3,2,1,0:T(8,128)(2,1)} %refs_5_.3, bf16[2,2,8,3072]{3,2,1,0:T(8,128)(2,1)S(1)} %copy-done.1, ...), custom_call_target="tpu_custom_call" | custom-call | flops 3000000000 | bytes 1600000 | tf_op jit(solution)/shard_map/pallas_call | solution.py:188
  41.0 7.8 %all-to-all-done.center = bf16[16,8,3072]{2,1,0:T(8,128)(2,1)S(1)} async-done(((bf16[16,8,3072]{2,1,0:T(8,128)(2,1)}), bf16[16,8,3072]{2,1,0:T(8,128)(2,1)S(1)}, u32[]{:S(2)}, u32[]{:S(2)}) %all-to-all-start) | async-done | bytes 786464 | tf_op jit(solution)/shard_map/all_to_all | solution.py:436
  48.8 2.1 %looks.1.own = f32[192,128]{1,0:T(8,128)S(1)} custom-call(bf16[16,8,3072]{2,1,0:T(8,128)(2,1)S(1)} %all-to-all-done.center, f32[768,256]{1,0:T(8,128)S(1)} %get-tuple-element.29.near_first, f32[1536,256]{1,0:T(8,128)S(1)} %get-tuple-element.30.second, f32[208,64]{1,0:T(8,128)S(1)} %get-tuple-element.31.power0, f32[208,64]{1,0:T(8,128)S(1)} %get-tuple-element.32.power1, ...), custom_call_target="tpu_custom_call" | custom-call | tf_op jit(solution)/shard_map/looks/pallas_call | solution.py:244
  50.9 4.4 %collective-permute-start.12 = (f32[192,128]{1,0:T(8,128)S(1)}, f32[192,128]{1,0:T(8,128)S(1)}, u32[]{:S(2)}, u32[]{:S(2)}) collective-permute-start(f32[192,128]{1,0:T(8,128)S(1)} %looks.1.own), channel_id=1, source_target_pairs={{1,2},{2,1},{5,6},{6,5},{9,10},{10,9},{13,14},{14,13},{17,18},{18,... | collective-permute-start | bytes 294920 | tf_op jit(solution)/shard_map/ppermute | solution.py:79
  55.3 2.2 %collective-permute-done.12.other = f32[192,128]{1,0:T(8,128)S(1)} collective-permute-done((f32[192,128]{1,0:T(8,128)S(1)}, f32[192,128]{1,0:T(8,128)S(1)}, u32[]{:S(2)}, u32[]{:S(2)}) %collective-permute-start.12) | collective-permute-done | bytes 98336 | tf_op jit(solution)/shard_map/ppermute | solution.py:79
  58.1 16.4 %all_to_all.10.arrived = bf16[64,2,128]{2,1,0:T(2,128)(2,1)S(1)} all-to-all(bf16[64,2,128]{2,1,0:T(2,128)(2,1)S(1)} %coherence.1), channel_id=1, replica_groups=mesh['date'=64,'az'=4] {'date'}, dimensions={0} | all-to-all | bytes 65536 | tf_op jit(solution)/shard_map/all_to_all | solution.py:441
  74.6 1.3 %finish.1 = (bf16[96,128]{1,0:T(8,128)(2,1)}, f32[3,16]{1,0:T(4,128)}) custom-call(bf16[64,2,128]{2,1,0:T(2,128)(2,1)S(1)} %all_to_all.10.arrived), custom_call_target="tpu_custom_call" | custom-call | tf_op jit(solution)/shard_map/finish/pallas_call | solution.py:328
  (21 shorter events, 2.1 us)
Async XLA Ops:
  1.9 7.5 %collective-permute-start = (bf16[4,8,3072]{2,1,0:T(8,128)(2,1)S(1)}, bf16[4,8,3072]{2,1,0:T(8,128)(2,1)S(1)}, u32[]{:S(2)}, u32[]{:S(2)}) collective-permute-start(bf16[4,8,3072]{2,1,0:T(8,128)(2,1)S(1)} %get-tuple-element.20), channel_id=1, source_target_pairs={{0,16},{1,17},{2,18},{3,19}} | collective-permute-start | bytes 589832 | tf_op jit(solution)/shard_map/ppermute | solution.py:410
  5.9 5.5 %collective-permute-start.1 = (bf16[4,8,3072]{2,1,0:T(8,128)(2,1)S(1)}, bf16[4,8,3072]{2,1,0:T(8,128)(2,1)S(1)}, u32[]{:S(2)}, u32[]{:S(2)}) collective-permute-start(bf16[4,8,3072]{2,1,0:T(8,128)(2,1)S(1)} %get-tuple-element.21), channel_id=1, source_target_pairs={{0,48},{1,49},{2,50},{3,51}} | collective-permute-start | bytes 589832 | tf_op jit(solution)/shard_map/ppermute | solution.py:410
  7.8 4.9 %collective-permute-start.2 = (bf16[4,8,3072]{2,1,0:T(8,128)(2,1)S(1)}, bf16[4,8,3072]{2,1,0:T(8,128)(2,1)S(1)}, u32[]{:S(2)}, u32[]{:S(2)}) collective-permute-start(bf16[4,8,3072]{2,1,0:T(8,128)(2,1)S(1)} %get-tuple-element.22), channel_id=1, source_target_pairs={{0,4},{1,5},{2,6},{3,7}} | collective-permute-start | bytes 589832 | tf_op jit(solution)/shard_map/ppermute | solution.py:410
  12.7 10.0 %collective-permute-start.4 = (bf16[1,8,3072]{2,1,0:T(8,128)(2,1)S(1)}, bf16[1,8,3072]{2,1,0:T(8,128)(2,1)S(1)}, u32[]{:S(2)}, u32[]{:S(2)}) collective-permute-start(bf16[1,8,3072]{2,1,0:T(8,128)(2,1)S(1)} %get-tuple-element.38), channel_id=1, source_target_pairs={{0,28},{16,20},{48,56},{4,24},{1,29},{17,21},{49,57},{5,25},{2,30}... | collective-permute-start | bytes 147464 | tf_op jit(solution)/shard_map/ppermute | solution.py:417
  14.0 8.7 %collective-permute-start.5 = (bf16[1,8,3072]{2,1,0:T(8,128)(2,1)S(1)}, bf16[1,8,3072]{2,1,0:T(8,128)(2,1)S(1)}, u32[]{:S(2)}, u32[]{:S(2)}) collective-permute-start(bf16[1,8,3072]{2,1,0:T(8,128)(2,1)S(1)} %get-tuple-element.39), channel_id=1, source_target_pairs={{0,60},{16,36},{48,44},{4,40},{1,61},{17,37},{49,45},{5,41},{2,62}... | collective-permute-start | bytes 147464 | tf_op jit(solution)/shard_map/ppermute | solution.py:417
  15.3 7.5 %collective-permute-start.3 = (bf16[1,8,3072]{2,1,0:T(8,128)(2,1)S(1)}, bf16[1,8,3072]{2,1,0:T(8,128)(2,1)S(1)}, u32[]{:S(2)}, u32[]{:S(2)}) collective-permute-start(bf16[1,8,3072]{2,1,0:T(8,128)(2,1)S(1)} %get-tuple-element.40), channel_id=1, source_target_pairs={{0,12},{16,32},{48,52},{4,8},{1,13},{17,33},{49,53},{5,9},{2,14},{... | collective-permute-start | bytes 147464 | tf_op jit(solution)/shard_map/ppermute | solution.py:417
  17.7 9.0 %collective-permute-start.10 = (bf16[2,2,8,3072]{3,2,1,0:T(8,128)(2,1)S(1)}, bf16[2,2,8,3072]{3,2,1,0:T(8,128)(2,1)S(1)}, u32[]{:S(2)}, u32[]{:S(2)}) collective-permute-start(bf16[2,2,8,3072]{3,2,1,0:T(8,128)(2,1)S(1)} %get-tuple-element.36), channel_id=1, source_target_pairs={{1,2},{2,1},{5,6},{6,5},{9,10},{10,9},{13,14},{14,13},{17,18},{18,... | collective-permute-start | bytes 589832 | tf_op jit(solution)/shard_map/ppermute | solution.py:79
  22.7 4.1 %collective-permute-start.9 = (bf16[2,2,8,3072]{3,2,1,0:T(8,128)(2,1)S(1)}, bf16[2,2,8,3072]{3,2,1,0:T(8,128)(2,1)S(1)}, u32[]{:S(2)}, u32[]{:S(2)}) collective-permute-start(bf16[2,2,8,3072]{3,2,1,0:T(8,128)(2,1)S(1)} %get-tuple-element.37), channel_id=1, source_target_pairs={{0,1},{1,0},{2,3},{3,2},{4,5},{5,4},{6,7},{7,6},{8,9},{9,8},{10,11... | collective-permute-start | bytes 589832 | tf_op jit(solution)/shard_map/ppermute | solution.py:78
  22.8 8.5 %collective-permute-start.8 = (bf16[1,8,3072]{2,1,0:T(8,128)(2,1)S(1)}, bf16[1,8,3072]{2,1,0:T(8,128)(2,1)S(1)}, u32[]{:S(2)}, u32[]{:S(2)}) collective-permute-start(bf16[1,8,3072]{2,1,0:T(8,128)(2,1)S(1)} %slice_add_fusion.own), channel_id=1, source_target_pairs={{0,128},{12,140},{28,156},{60,188},{16,144},{32,160},{20,148},{36,... | collective-permute-start | bytes 147464 | tf_op jit(solution)/shard_map/ppermute | solution.py:428
  24.1 7.2 %collective-permute-start.7 = (bf16[1,8,3072]{2,1,0:T(8,128)(2,1)S(1)}, bf16[1,8,3072]{2,1,0:T(8,128)(2,1)S(1)}, u32[]{:S(2)}, u32[]{:S(2)}) collective-permute-start(bf16[1,8,3072]{2,1,0:T(8,128)(2,1)S(1)} %slice_add_fusion.own), channel_id=1, source_target_pairs={{0,192},{12,204},{28,220},{60,252},{16,208},{32,224},{20,212},{36,... | collective-permute-start | bytes 147464 | tf_op jit(solution)/shard_map/ppermute | solution.py:428
  25.4 5.9 %collective-permute-start.6 = (bf16[1,8,3072]{2,1,0:T(8,128)(2,1)S(1)}, bf16[1,8,3072]{2,1,0:T(8,128)(2,1)S(1)}, u32[]{:S(2)}, u32[]{:S(2)}) collective-permute-start(bf16[1,8,3072]{2,1,0:T(8,128)(2,1)S(1)} %slice_add_fusion.own), channel_id=1, source_target_pairs={{0,64},{12,76},{28,92},{60,124},{16,80},{32,96},{20,84},{36,100},{... | collective-permute-start | bytes 147464 | tf_op jit(solution)/shard_map/ppermute | solution.py:428
  26.7 4.5 %copy-start = (bf16[2,2,8,3072]{3,2,1,0:T(8,128)(2,1)}, bf16[2,2,8,3072]{3,2,1,0:T(8,128)(2,1)S(1)}, u32[]{:S(2)}) copy-start(bf16[2,2,8,3072]{3,2,1,0:T(8,128)(2,1)S(1)} %collective-permute-done.9.refs_6_) | copy-start | bytes 589828
  32.4 16.4 %all-to-all-start = ((bf16[16,8,3072]{2,1,0:T(8,128)(2,1)}), bf16[16,8,3072]{2,1,0:T(8,128)(2,1)S(1)}, u32[]{:S(2)}, u32[]{:S(2)}) async-start(bf16[16,8,3072]{2,1,0:T(8,128)(2,1)} %copies.1), calls=%async_computation | async-start | bytes 1572864 | tf_op jit(solution)/shard_map/all_to_all | solution.py:436
  36.0 0.9 %copy-start.1 = (bf16[2,2,8,3072]{3,2,1,0:T(8,128)(2,1)S(1)}, bf16[2,2,8,3072]{3,2,1,0:T(8,128)(2,1)}, u32[]{:S(2)}) copy-start(bf16[2,2,8,3072]{3,2,1,0:T(8,128)(2,1)} %copy-done) | copy-start | bytes 589828
  50.9 6.7 %collective-permute-start.12 = (f32[192,128]{1,0:T(8,128)S(1)}, f32[192,128]{1,0:T(8,128)S(1)}, u32[]{:S(2)}, u32[]{:S(2)}) collective-permute-start(f32[192,128]{1,0:T(8,128)S(1)} %looks.1.own), channel_id=1, source_target_pairs={{1,2},{2,1},{5,6},{6,5},{9,10},{10,9},{13,14},{14,13},{17,18},{18,... | collective-permute-start | bytes 294920 | tf_op jit(solution)/shard_map/ppermute | solution.py:79
  55.2 2.3 %collective-permute-start.11 = (f32[192,128]{1,0:T(8,128)S(1)}, f32[192,128]{1,0:T(8,128)S(1)}, u32[]{:S(2)}, u32[]{:S(2)}) collective-permute-start(f32[192,128]{1,0:T(8,128)S(1)} %looks.1.own), channel_id=1, source_target_pairs={{0,1},{1,0},{2,3},{3,2},{4,5},{5,4},{6,7},{7,6},{8,9},{9,8},{10,11... | collective-permute-start | bytes 294920 | tf_op jit(solution)/shard_map/ppermute | solution.py:78

commit v3 on v2

--- a/solution.py
+++ b/solution.py
@@ -74,10 +74,9 @@
 
 
 def swapped(to_partner, to_other):
-    return (
-        lax.ppermute(to_partner, "az", [(0, 1), (1, 0), (2, 3), (3, 2)]),
-        lax.ppermute(to_other, "az", [(1, 2), (2, 1)]),
-    )
+    partner = lax.ppermute(to_partner, "az", [(0, 1), (1, 0), (2, 3), (3, 2)])
+    other = lax.ppermute(to_other, "az", [(1, 2), (2, 1)])
+    return partner, other
 
 
 def resample_kernel(
@@ -339,14 +338,23 @@
 
 
 def quarters_kernel(slc, *rest):
-    *outs, arrived = rest
+    *outs, to_partner, to_other, arrived = rest
+    odd = odd_block()
     copies = []
-    for out, homes in zip(outs, HOMES):
-        for at, (x, y) in enumerate(homes):
-            part, block = divmod(x * 4 + y, 8)
-            source = slc.at[0, part, pl.ds(block * 8, 8)]
+    for out, start in (
+        (to_partner, jnp.where(odd, 0, ROWS - 8)),
+        (to_other, jnp.where(odd, ROWS - 8, 0)),
+    ):
+        source = slc.at[:, :, pl.ds(pl.multiple_of(start, 8), 8)]
+        copies.append(pltpu.make_async_copy(source, out, arrived.at[len(copies)]))
+    for out, *pair in zip(outs, *HOMES):
+        for at, homes in enumerate(zip(*pair)):
+            even_index, odd_index = [x * 4 + y for x, y in homes]
+            index = jnp.where(odd, odd_index, even_index)
+            part, block = lax.div(index, 8), lax.rem(index, 8)
+            source = slc.at[0, part, pl.ds(pl.multiple_of(block * 8, 8), 8)]
             copies.append(pltpu.make_async_copy(source, out.at[at], arrived.at[len(copies)]))
-    for copy in copies:
+    for copy in copies[2:] + copies[:2]:
         copy.start()
     for copy in copies:
         copy.wait()
@@ -357,10 +365,10 @@
         quarters_kernel,
         name="quarters",
         compiler_params=GRANT,
-        out_shape=(VMEM((4, 8, COLS), BF16),) * 4,
+        out_shape=(VMEM((4, 8, COLS), BF16),) * 4 + (VMEM((2, 2, 8, COLS), BF16),) * 2,
         in_specs=[pl.BlockSpec(memory_space=pl.ANY)],
-        out_specs=(pl.BlockSpec(memory_space=VMEM),) * 4,
-        scratch_shapes=[pltpu.SemaphoreType.DMA((16,))],
+        out_specs=(pl.BlockSpec(memory_space=VMEM),) * 6,
+        scratch_shapes=[pltpu.SemaphoreType.DMA((18,))],
     )(*far_away(slc))
 
 
@@ -393,37 +401,47 @@
     return z * 16 + x * 4 + y
 
 
-HOMES = (
+EVEN = (
     ((0, 0), (0, 3), (1, 3), (3, 3)),
     ((1, 0), (2, 0), (1, 1), (2, 1)),
     ((3, 0), (3, 1), (3, 2), (2, 3)),
     ((0, 1), (0, 2), (1, 2), (2, 2)),
 )
+HOMES = (EVEN, tuple(tuple((y, -x % 4) for x, y in homes) for homes in EVEN))
+
+
+def send(value, hops):
+    pairs = [
+        (place(0, *source) * 4 + az, place(0, *target) * 4 + az)
+        for az in range(4)
+        for source, target in hops[az % 2]
+    ]
+    return lax.ppermute(value, ("date", "az"), pairs)
 
 
 def body(slc, az_shift, rg_shift, az_frac, rg_frac):
     scalars = (az_shift, rg_shift, az_frac, rg_frac, jnp.asarray(kernel_bank()))
-    quarters = quarters_of(slc)
+    *quarters, to_partner, to_other = quarters_of(slc)
     kept = jnp.where(lax.axis_index("date") == 0, quarters[0], jnp.zeros_like(quarters[0]))
     kept = lax.optimization_barrier(kept)
 
-    pieces = [lax.ppermute(quarters[k], "date", [(0, place(0, *HOMES[k][0]))]) for k in range(1, 4)]
-    head, tail = slc[:, :, :8], slc[:, :, ROWS - 8 :]
-    odd = odd_block()
-    edges = swapped(jnp.where(odd, head, tail), jnp.where(odd, tail, head))
+    pieces = [
+        send(quarters[k], [[(homes[0][0], homes[k][0])] for homes in HOMES])
+        for k in range(1, 4)
+    ]
+    edges = swapped(to_partner, to_other)
     quarter = kept + sum(pieces)
 
     pieces = [
-        lax.ppermute(
+        send(
             quarter[k : k + 1],
-            "date",
-            [(place(0, *homes[0]), place(0, *homes[k])) for homes in HOMES],
+            [[(group[0], group[k]) for group in homes] for homes in HOMES],
         )
         for k in range(1, 4)
     ]
     chunk = quarter[0:1] + sum(pieces)
 
-    flat = [home for homes in HOMES for home in homes]
+    flat = [home for group in EVEN for home in group]
     pieces = [
         lax.ppermute(chunk, "date", [(place(0, *home), place(k, *home)) for home in flat])
         for k in (1, 3, 2)
@@ -437,7 +455,8 @@
     near_first, far_first, power0 = first
     second, power1 = resample(1, False, scalars, slc, *edges)
     own = looks(center, near_first, far_first, second, power0, power1)
-    outgoing = coherence(own, *swapped(own, own))
+    around = swapped(own, own)
+    outgoing = coherence(own, *around)
     arrived = lax.all_to_all(outgoing, "date", split_axis=0, concat_axis=0, tiled=True)
     rows, mean = finish(arrived)
     return rows.reshape(3, LOOKS, 2, 128), mean

time: 76.5 us -> 74.8 us (0.978)
  the two profiles are of different devices: /device:TPU:1 before, /device:TPU:32 now
where the time goes in v3:
time: 74.8 us; the launch traced here: 73.9 us
  starting transfers between devices  24.3 us (32%)
  waiting for transfers between devices  16.4 us (22%)
  blocking collectives  16.2 us (22%)
  Pallas kernels  15 us (20%)
  local copies, waits for them, and re-layouts  0.94 us (1%)
  between operations  0.9 us (1%)
    all_to_all x1, blocking collectives, body(): lax.all_to_all(outgoing, 'date', split_axis=0, concat_axis=0, tiled=True)  16.2 us
    ppermute x6, starting transfers between devices, send(): return lax.ppermute(value, ('date', 'az'), pairs)  10.5 us
    pallas_call x2, Pallas kernels, resample(): pl.pallas_call(functools.partial(resample_kernel, date, len(spaces)), com...  8.49 us
    all_to_all x1, waiting for transfers between devices, body(): lax.all_to_all(copies, 'date', 0, 0, axis_index_groups=planes, tiled=True)  7.68 us
    all_to_all x1, starting transfers between devices, body(): lax.all_to_all(copies, 'date', 0, 0, axis_index_groups=planes, tiled=True)  5.71 us
    ppermute x2, waiting for transfers between devices, swapped(): other = lax.ppermute(to_other, 'az', [(1, 2), (2, 1)])  5.07 us
    ppermute x2, starting transfers between devices, swapped(): other = lax.ppermute(to_other, 'az', [(1, 2), (2, 1)])  4.03 us
    ppermute x3, starting transfers between devices, body(): lax.ppermute(chunk, 'date', [(place(0, *home), place(k, *home)) for home...  3.88 us
  transfers between devices with their start and end apart: 14, of which 5 were waited for; matrix products, arithmetic and copies ran while one was open for 0% of the time, Pallas kernels for 11%

profile of v3, /device:TPU:32, one launch (start us, length us, event | category | flops | bytes accessed | tf_op | source)
XLA Modules:
  0.0 73.9 jit_solution(15854459428478038999)
XLA Ops:
  0.6 1.5 %quarters.1 = (bf16[4,8,3072]{2,1,0:T(8,128)(2,1)S(1)}, bf16[4,8,3072]{2,1,0:T(8,128)(2,1)S(1)}, bf16[4,8,3072]{2,1,0:T(8,128)(2,1)S(1)}, bf16[4,8,3072]{2,1,0:T...) custom-call(bf16[2,2,64,3072]{3,2,1,0:T(8,128)(2,1)} %refs_5_.3), custom_call_target="tpu_custom_call" | custom-call | tf_op jit(solution)/shard_map/quarters/pallas_call | solution.py:364
  2.2 3.4 %collective-permute-start = (bf16[4,8,3072]{2,1,0:T(8,128)(2,1)S(1)}, bf16[4,8,3072]{2,1,0:T(8,128)(2,1)S(1)}, u32[]{:S(2)}, u32[]{:S(2)}) collective-permute-start(bf16[4,8,3072]{2,1,0:T(8,128)(2,1)S(1)} %get-tuple-element.22), channel_id=1, source_target_pairs={{0,16},{1,13},{2,18},{3,15}} | collective-permute-start | bytes 589832 | tf_op jit(solution)/shard_map/ppermute | solution.py:419
  5.6 1.9 %collective-permute-start.1 = (bf16[4,8,3072]{2,1,0:T(8,128)(2,1)S(1)}, bf16[4,8,3072]{2,1,0:T(8,128)(2,1)S(1)}, u32[]{:S(2)}, u32[]{:S(2)}) collective-permute-start(bf16[4,8,3072]{2,1,0:T(8,128)(2,1)S(1)} %get-tuple-element.23), channel_id=1, source_target_pairs={{0,48},{1,5},{2,50},{3,7}} | collective-permute-start | bytes 589832 | tf_op jit(solution)/shard_map/ppermute | solution.py:419
  7.5 1.3 %collective-permute-start.2 = (bf16[4,8,3072]{2,1,0:T(8,128)(2,1)S(1)}, bf16[4,8,3072]{2,1,0:T(8,128)(2,1)S(1)}, u32[]{:S(2)}, u32[]{:S(2)}) collective-permute-start(bf16[4,8,3072]{2,1,0:T(8,128)(2,1)S(1)} %get-tuple-element.24), channel_id=1, source_target_pairs={{0,4},{1,17},{2,6},{3,19}} | collective-permute-start | bytes 589832 | tf_op jit(solution)/shard_map/ppermute | solution.py:419
  8.9 1.8 %collective-permute-done.1 = bf16[4,8,3072]{2,1,0:T(8,128)(2,1)S(1)} collective-permute-done((bf16[4,8,3072]{2,1,0:T(8,128)(2,1)S(1)}, bf16[4,8,3072]{2,1,0:T(8,128)(2,1)S(1)}, u32[]{:S(2)}, u32[]{:S(2)}) %collective-permute-start.1) | collective-permute-done | bytes 196640 | tf_op jit(solution)/shard_map/ppermute | solution.py:419
  10.7 1.9 %collective-permute-done.2 = bf16[4,8,3072]{2,1,0:T(8,128)(2,1)S(1)} collective-permute-done((bf16[4,8,3072]{2,1,0:T(8,128)(2,1)S(1)}, bf16[4,8,3072]{2,1,0:T(8,128)(2,1)S(1)}, u32[]{:S(2)}, u32[]{:S(2)}) %collective-permute-start.2) | collective-permute-done | bytes 196640 | tf_op jit(solution)/shard_map/ppermute | solution.py:419
  12.6 1.3 %collective-permute-start.4 = (bf16[1,8,3072]{2,1,0:T(8,128)(2,1)S(1)}, bf16[1,8,3072]{2,1,0:T(8,128)(2,1)S(1)}, u32[]{:S(2)}, u32[]{:S(2)}) collective-permute-start(bf16[1,8,3072]{2,1,0:T(8,128)(2,1)S(1)} %get-tuple-element.40), channel_id=1, source_target_pairs={{0,28},{16,20},{48,56},{4,24},{1,61},{13,29},{5,37},{17,45},{2,30}... | collective-permute-start | bytes 147464 | tf_op jit(solution)/shard_map/ppermute | solution.py:419
  13.9 1.3 %collective-permute-start.5 = (bf16[1,8,3072]{2,1,0:T(8,128)(2,1)S(1)}, bf16[1,8,3072]{2,1,0:T(8,128)(2,1)S(1)}, u32[]{:S(2)}, u32[]{:S(2)}) collective-permute-start(bf16[1,8,3072]{2,1,0:T(8,128)(2,1)S(1)} %get-tuple-element.41), channel_id=1, source_target_pairs={{0,60},{16,36},{48,44},{4,40},{1,53},{13,25},{5,57},{17,41},{2,62}... | collective-permute-start | bytes 147464 | tf_op jit(solution)/shard_map/ppermute | solution.py:419
  15.2 1.3 %collective-permute-start.3 = (bf16[1,8,3072]{2,1,0:T(8,128)(2,1)S(1)}, bf16[1,8,3072]{2,1,0:T(8,128)(2,1)S(1)}, u32[]{:S(2)}, u32[]{:S(2)}) collective-permute-start(bf16[1,8,3072]{2,1,0:T(8,128)(2,1)S(1)} %get-tuple-element.42), channel_id=1, source_target_pairs={{0,12},{16,32},{48,52},{4,8},{1,49},{13,9},{5,21},{17,33},{2,14},{... | collective-permute-start | bytes 147464 | tf_op jit(solution)/shard_map/ppermute | solution.py:419
  16.6 2.1 %collective-permute-start.10 = (bf16[2,2,8,3072]{3,2,1,0:T(8,128)(2,1)S(1)}, bf16[2,2,8,3072]{3,2,1,0:T(8,128)(2,1)S(1)}, u32[]{:S(2)}, u32[]{:S(2)}) collective-permute-start(bf16[2,2,8,3072]{3,2,1,0:T(8,128)(2,1)S(1)} %get-tuple-element.26), channel_id=1, source_target_pairs={{1,2},{2,1},{5,6},{6,5},{9,10},{10,9},{13,14},{14,13},{17,18},{18,... | collective-permute-start | bytes 589832 | tf_op jit(solution)/shard_map/ppermute | solution.py:78
  18.8 1.3 %collective-permute-start.8 = (bf16[1,8,3072]{2,1,0:T(8,128)(2,1)S(1)}, bf16[1,8,3072]{2,1,0:T(8,128)(2,1)S(1)}, u32[]{:S(2)}, u32[]{:S(2)}) collective-permute-start(bf16[1,8,3072]{2,1,0:T(8,128)(2,1)S(1)} %slice_add_fusion.own), channel_id=1, source_target_pairs={{0,128},{12,140},{28,156},{60,188},{16,144},{32,160},{20,148},{36,... | collective-permute-start | bytes 147464 | tf_op jit(solution)/shard_map/ppermute | solution.py:446
  20.1 1.3 %collective-permute-start.7 = (bf16[1,8,3072]{2,1,0:T(8,128)(2,1)S(1)}, bf16[1,8,3072]{2,1,0:T(8,128)(2,1)S(1)}, u32[]{:S(2)}, u32[]{:S(2)}) collective-permute-start(bf16[1,8,3072]{2,1,0:T(8,128)(2,1)S(1)} %slice_add_fusion.own), channel_id=1, source_target_pairs={{0,192},{12,204},{28,220},{60,252},{16,208},{32,224},{20,212},{36,... | collective-permute-start | bytes 147464 | tf_op jit(solution)/shard_map/ppermute | solution.py:446
  21.4 1.3 %collective-permute-start.6 = (bf16[1,8,3072]{2,1,0:T(8,128)(2,1)S(1)}, bf16[1,8,3072]{2,1,0:T(8,128)(2,1)S(1)}, u32[]{:S(2)}, u32[]{:S(2)}) collective-permute-start(bf16[1,8,3072]{2,1,0:T(8,128)(2,1)S(1)} %slice_add_fusion.own), channel_id=1, source_target_pairs={{0,64},{12,76},{28,92},{60,124},{16,80},{32,96},{20,84},{36,100},{... | collective-permute-start | bytes 147464 | tf_op jit(solution)/shard_map/ppermute | solution.py:446
  22.7 1.2 %collective-permute-done.10.refs_7_ = bf16[2,2,8,3072]{3,2,1,0:T(8,128)(2,1)S(1)} collective-permute-done((bf16[2,2,8,3072]{3,2,1,0:T(8,128)(2,1)S(1)}, bf16[2,2,8,3072]{3,2,1,0:T(8,128)(2,1)S(1)}, u32[]{:S(2)}, u32[]{:S(2)}) %collective-permute-start.10) | collective-permute-done | bytes 196640 | tf_op jit(solution)/shard_map/ppermute | solution.py:78
  23.9 4.5 %shard_map.77 = (f32[768,256]{1,0:T(8,128)S(1)}, f32[768,256]{1,0:T(8,128)}, f32[208,64]{1,0:T(8,128)S(1)}) custom-call(s32[2]{0:T(128)} %refs_0_.3, s32[2]{0:T(128)} %refs_1_.3, s32[2]{0:T(128)} %refs_2_.3, s32[2]{0:T(128)} %refs_3_.3, f32[16,8]{1,0:T(8,128)} %constant.12.clone.refs_4_, bf16[2,2,64,3072]{3,2,1,0:T(8,128)(2,1)} %refs_5_.3, ...), custom_call_target="tpu_custom_call" | custom-call | flops 3000000000 | bytes 1600000 | tf_op jit(solution)/shard_map/pallas_call | solution.py:187
  28.4 1.1 %copies.1 = bf16[16,8,3072]{2,1,0:T(8,128)(2,1)} custom-call(bf16[1,8,3072]{2,1,0:T(8,128)(2,1)S(1)} %slice_add_fusion.own, bf16[1,8,3072]{2,1,0:T(8,128)(2,1)S(1)} %collective-permute-done.6.rest_0_, bf16[1,8,3072]{2,1,0:T(8,128)(2,1)S(1)} %collective-permute-done.7.rest_1_, bf16[1,8,3072]{2,1,0:T(8,128)(2,1)S(1)} %collective-permute-done.8.rest_2_), custom_call_target="tpu_custom_call" | custom-call | tf_op jit(solution)/shard_map/copies/pallas_call | solution.py:389
  29.5 5.7 %all-to-all-start = ((bf16[16,8,3072]{2,1,0:T(8,128)(2,1)}), bf16[16,8,3072]{2,1,0:T(8,128)(2,1)S(1)}, u32[]{:S(2)}, u32[]{:S(2)}) async-start(bf16[16,8,3072]{2,1,0:T(8,128)(2,1)} %copies.1), calls=%async_computation | async-start | bytes 1572864 | tf_op jit(solution)/shard_map/all_to_all | solution.py:454
  36.1 4.0 %shard_map.78 = (f32[1536,256]{1,0:T(8,128)S(1)}, f32[208,64]{1,0:T(8,128)S(1)}) custom-call(s32[2]{0:T(128)} %refs_0_.3, s32[2]{0:T(128)} %refs_1_.3, s32[2]{0:T(128)} %refs_2_.3, s32[2]{0:T(128)} %refs_3_.3, f32[16,8]{1,0:T(8,128)} %constant.12.clone.refs_4_, bf16[2,2,64,3072]{3,2,1,0:T(8,128)(2,1)} %refs_5_.3, ...), custom_call_target="tpu_custom_call" | custom-call | flops 3000000000 | bytes 1600000 | tf_op jit(solution)/shard_map/pallas_call | solution.py:187
  40.2 7.7 %all-to-all-done.center = bf16[16,8,3072]{2,1,0:T(8,128)(2,1)S(1)} async-done(((bf16[16,8,3072]{2,1,0:T(8,128)(2,1)}), bf16[16,8,3072]{2,1,0:T(8,128)(2,1)S(1)}, u32[]{:S(2)}, u32[]{:S(2)}) %all-to-all-start) | async-done | bytes 786464 | tf_op jit(solution)/shard_map/all_to_all | solution.py:454
  47.8 2.1 %looks.1.own = f32[192,128]{1,0:T(8,128)S(1)} custom-call(bf16[16,8,3072]{2,1,0:T(8,128)(2,1)S(1)} %all-to-all-done.center, f32[768,256]{1,0:T(8,128)S(1)} %get-tuple-element.33.near_first, f32[1536,256]{1,0:T(8,128)S(1)} %get-tuple-element.34.second, f32[208,64]{1,0:T(8,128)S(1)} %get-tuple-element.35.power0, f32[208,64]{1,0:T(8,128)S(1)} %get-tuple-element.36.power1, ...), custom_call_target="tpu_custom_call" | custom-call | tf_op jit(solution)/shard_map/looks/pallas_call | solution.py:243
  49.9 1.9 %collective-permute-start.12 = (f32[192,128]{1,0:T(8,128)S(1)}, f32[192,128]{1,0:T(8,128)S(1)}, u32[]{:S(2)}, u32[]{:S(2)}) collective-permute-start(f32[192,128]{1,0:T(8,128)S(1)} %looks.1.own), channel_id=1, source_target_pairs={{1,2},{2,1},{5,6},{6,5},{9,10},{10,9},{13,14},{14,13},{17,18},{18,... | collective-permute-start | bytes 294920 | tf_op jit(solution)/shard_map/ppermute | solution.py:78
  51.9 3.9 %collective-permute-done.12.other = f32[192,128]{1,0:T(8,128)S(1)} collective-permute-done((f32[192,128]{1,0:T(8,128)S(1)}, f32[192,128]{1,0:T(8,128)S(1)}, u32[]{:S(2)}, u32[]{:S(2)}) %collective-permute-start.12) | collective-permute-done | bytes 98336 | tf_op jit(solution)/shard_map/ppermute | solution.py:78
  56.5 16.2 %all_to_all.10.arrived = bf16[64,2,128]{2,1,0:T(2,128)(2,1)S(1)} all-to-all(bf16[64,2,128]{2,1,0:T(2,128)(2,1)S(1)} %coherence.1), channel_id=1, replica_groups=mesh['date'=64,'az'=4] {'date'}, dimensions={0} | all-to-all | bytes 65536 | tf_op jit(solution)/shard_map/all_to_all | solution.py:460
  72.6 1.3 %finish.1 = (bf16[96,128]{1,0:T(8,128)(2,1)}, f32[3,16]{1,0:T(4,128)}) custom-call(bf16[64,2,128]{2,1,0:T(2,128)(2,1)S(1)} %all_to_all.10.arrived), custom_call_target="tpu_custom_call" | custom-call | tf_op jit(solution)/shard_map/finish/pallas_call | solution.py:327
  (20 shorter events, 1.8 us)
Async XLA Ops:
  2.2 6.7 %collective-permute-start = (bf16[4,8,3072]{2,1,0:T(8,128)(2,1)S(1)}, bf16[4,8,3072]{2,1,0:T(8,128)(2,1)S(1)}, u32[]{:S(2)}, u32[]{:S(2)}) collective-permute-start(bf16[4,8,3072]{2,1,0:T(8,128)(2,1)S(1)} %get-tuple-element.22), channel_id=1, source_target_pairs={{0,16},{1,13},{2,18},{3,15}} | collective-permute-start | bytes 589832 | tf_op jit(solution)/shard_map/ppermute | solution.py:419
  5.6 5.1 %collective-permute-start.1 = (bf16[4,8,3072]{2,1,0:T(8,128)(2,1)S(1)}, bf16[4,8,3072]{2,1,0:T(8,128)(2,1)S(1)}, u32[]{:S(2)}, u32[]{:S(2)}) collective-permute-start(bf16[4,8,3072]{2,1,0:T(8,128)(2,1)S(1)} %get-tuple-element.23), channel_id=1, source_target_pairs={{0,48},{1,5},{2,50},{3,7}} | collective-permute-start | bytes 589832 | tf_op jit(solution)/shard_map/ppermute | solution.py:419
  7.5 5.0 %collective-permute-start.2 = (bf16[4,8,3072]{2,1,0:T(8,128)(2,1)S(1)}, bf16[4,8,3072]{2,1,0:T(8,128)(2,1)S(1)}, u32[]{:S(2)}, u32[]{:S(2)}) collective-permute-start(bf16[4,8,3072]{2,1,0:T(8,128)(2,1)S(1)} %get-tuple-element.24), channel_id=1, source_target_pairs={{0,4},{1,17},{2,6},{3,19}} | collective-permute-start | bytes 589832 | tf_op jit(solution)/shard_map/ppermute | solution.py:419
  12.6 6.1 %collective-permute-start.4 = (bf16[1,8,3072]{2,1,0:T(8,128)(2,1)S(1)}, bf16[1,8,3072]{2,1,0:T(8,128)(2,1)S(1)}, u32[]{:S(2)}, u32[]{:S(2)}) collective-permute-start(bf16[1,8,3072]{2,1,0:T(8,128)(2,1)S(1)} %get-tuple-element.40), channel_id=1, source_target_pairs={{0,28},{16,20},{48,56},{4,24},{1,61},{13,29},{5,37},{17,45},{2,30}... | collective-permute-start | bytes 147464 | tf_op jit(solution)/shard_map/ppermute | solution.py:419
  13.9 4.8 %collective-permute-start.5 = (bf16[1,8,3072]{2,1,0:T(8,128)(2,1)S(1)}, bf16[1,8,3072]{2,1,0:T(8,128)(2,1)S(1)}, u32[]{:S(2)}, u32[]{:S(2)}) collective-permute-start(bf16[1,8,3072]{2,1,0:T(8,128)(2,1)S(1)} %get-tuple-element.41), channel_id=1, source_target_pairs={{0,60},{16,36},{48,44},{4,40},{1,53},{13,25},{5,57},{17,41},{2,62}... | collective-permute-start | bytes 147464 | tf_op jit(solution)/shard_map/ppermute | solution.py:419
  15.2 3.5 %collective-permute-start.3 = (bf16[1,8,3072]{2,1,0:T(8,128)(2,1)S(1)}, bf16[1,8,3072]{2,1,0:T(8,128)(2,1)S(1)}, u32[]{:S(2)}, u32[]{:S(2)}) collective-permute-start(bf16[1,8,3072]{2,1,0:T(8,128)(2,1)S(1)} %get-tuple-element.42), channel_id=1, source_target_pairs={{0,12},{16,32},{48,52},{4,8},{1,49},{13,9},{5,21},{17,33},{2,14},{... | collective-permute-start | bytes 147464 | tf_op jit(solution)/shard_map/ppermute | solution.py:419
  16.5 6.2 %collective-permute-start.9 = (bf16[2,2,8,3072]{3,2,1,0:T(8,128)(2,1)S(1)}, bf16[2,2,8,3072]{3,2,1,0:T(8,128)(2,1)S(1)}, u32[]{:S(2)}, u32[]{:S(2)}) collective-permute-start(bf16[2,2,8,3072]{3,2,1,0:T(8,128)(2,1)S(1)} %get-tuple-element.25), channel_id=1, source_target_pairs={{0,1},{1,0},{2,3},{3,2},{4,5},{5,4},{6,7},{7,6},{8,9},{9,8},{10,11... | collective-permute-start | bytes 589832 | tf_op jit(solution)/shard_map/ppermute | solution.py:77
  16.6 7.2 %collective-permute-start.10 = (bf16[2,2,8,3072]{3,2,1,0:T(8,128)(2,1)S(1)}, bf16[2,2,8,3072]{3,2,1,0:T(8,128)(2,1)S(1)}, u32[]{:S(2)}, u32[]{:S(2)}) collective-permute-start(bf16[2,2,8,3072]{3,2,1,0:T(8,128)(2,1)S(1)} %get-tuple-element.26), channel_id=1, source_target_pairs={{1,2},{2,1},{5,6},{6,5},{9,10},{10,9},{13,14},{14,13},{17,18},{18,... | collective-permute-start | bytes 589832 | tf_op jit(solution)/shard_map/ppermute | solution.py:78
  18.8 9.6 %collective-permute-start.8 = (bf16[1,8,3072]{2,1,0:T(8,128)(2,1)S(1)}, bf16[1,8,3072]{2,1,0:T(8,128)(2,1)S(1)}, u32[]{:S(2)}, u32[]{:S(2)}) collective-permute-start(bf16[1,8,3072]{2,1,0:T(8,128)(2,1)S(1)} %slice_add_fusion.own), channel_id=1, source_target_pairs={{0,128},{12,140},{28,156},{60,188},{16,144},{32,160},{20,148},{36,... | collective-permute-start | bytes 147464 | tf_op jit(solution)/shard_map/ppermute | solution.py:446
  20.1 8.3 %collective-permute-start.7 = (bf16[1,8,3072]{2,1,0:T(8,128)(2,1)S(1)}, bf16[1,8,3072]{2,1,0:T(8,128)(2,1)S(1)}, u32[]{:S(2)}, u32[]{:S(2)}) collective-permute-start(bf16[1,8,3072]{2,1,0:T(8,128)(2,1)S(1)} %slice_add_fusion.own), channel_id=1, source_target_pairs={{0,192},{12,204},{28,220},{60,252},{16,208},{32,224},{20,212},{36,... | collective-permute-start | bytes 147464 | tf_op jit(solution)/shard_map/ppermute | solution.py:446
  21.4 7.0 %collective-permute-start.6 = (bf16[1,8,3072]{2,1,0:T(8,128)(2,1)S(1)}, bf16[1,8,3072]{2,1,0:T(8,128)(2,1)S(1)}, u32[]{:S(2)}, u32[]{:S(2)}) collective-permute-start(bf16[1,8,3072]{2,1,0:T(8,128)(2,1)S(1)} %slice_add_fusion.own), channel_id=1, source_target_pairs={{0,64},{12,76},{28,92},{60,124},{16,80},{32,96},{20,84},{36,100},{... | collective-permute-start | bytes 147464 | tf_op jit(solution)/shard_map/ppermute | solution.py:446
  23.9 4.5 %copy-start = (bf16[2,2,8,3072]{3,2,1,0:T(8,128)(2,1)}, bf16[2,2,8,3072]{3,2,1,0:T(8,128)(2,1)S(1)}, u32[]{:S(2)}) copy-start(bf16[2,2,8,3072]{3,2,1,0:T(8,128)(2,1)S(1)} %collective-permute-done.10.refs_7_) | copy-start | bytes 589828
  29.5 18.3 %all-to-all-start = ((bf16[16,8,3072]{2,1,0:T(8,128)(2,1)}), bf16[16,8,3072]{2,1,0:T(8,128)(2,1)S(1)}, u32[]{:S(2)}, u32[]{:S(2)}) async-start(bf16[16,8,3072]{2,1,0:T(8,128)(2,1)} %copies.1), calls=%async_computation | async-start | bytes 1572864 | tf_op jit(solution)/shard_map/all_to_all | solution.py:454
  35.2 0.9 %copy-start.1 = (bf16[2,2,8,3072]{3,2,1,0:T(8,128)(2,1)S(1)}, bf16[2,2,8,3072]{3,2,1,0:T(8,128)(2,1)}, u32[]{:S(2)}) copy-start(bf16[2,2,8,3072]{3,2,1,0:T(8,128)(2,1)} %copy-done) | copy-start | bytes 589828
  49.9 5.9 %collective-permute-start.12 = (f32[192,128]{1,0:T(8,128)S(1)}, f32[192,128]{1,0:T(8,128)S(1)}, u32[]{:S(2)}, u32[]{:S(2)}) collective-permute-start(f32[192,128]{1,0:T(8,128)S(1)} %looks.1.own), channel_id=1, source_target_pairs={{1,2},{2,1},{5,6},{6,5},{9,10},{10,9},{13,14},{14,13},{17,18},{18,... | collective-permute-start | bytes 294920 | tf_op jit(solution)/shard_map/ppermute | solution.py:78
  51.8 4.0 %collective-permute-start.11 = (f32[192,128]{1,0:T(8,128)S(1)}, f32[192,128]{1,0:T(8,128)S(1)}, u32[]{:S(2)}, u32[]{:S(2)}) collective-permute-start(f32[192,128]{1,0:T(8,128)S(1)} %looks.1.own), channel_id=1, source_target_pairs={{0,1},{1,0},{2,3},{3,2},{4,5},{5,4},{6,7},{7,6},{8,9},{9,8},{10,11... | collective-permute-start | bytes 294920 | tf_op jit(solution)/shard_map/ppermute | solution.py:77

commit v4 on v3

--- a/solution.py
+++ b/solution.py
@@ -93,7 +93,7 @@
     ]
     for load in loads:
         load.start()
-    azs, rgs, azf, rgf, bank = local
+    azs, rgs, azf, rgf, bank, *held = local
     copies = [
         pltpu.make_async_copy(source.at[date], edges.at[at], arrived.at[2 + at])
         for at, source in enumerate((partner, other))
@@ -148,17 +148,24 @@
                 if tile > 0:
                     at = (tile - 1) * 2 * ROWS + place
                     wide[at : at + ROWS, TILE : 2 * TILE] = piece
-    at = 0
-    for stack in stacks:
-        size = stack.shape[0]
+    far_copies = [
+        pltpu.make_async_copy(here, out, arrived.at[9]) for here, out in zip(held, stacks[1:])
+    ]
+    stacks = [stacks[0], *held]
+    size = stacks[0].shape[0]
+    for half_of in reversed(range(count)):
+        at = half_of * size
         hi, lo = wide_hi[at : at + size], wide_lo[at : at + size]
-        stack[...] = dot(hi, rg_hi) + (dot(lo, rg_hi) + dot(hi, rg_lo))
-        at += size
+        stacks[half_of][...] = dot(hi, rg_hi) + (dot(lo, rg_hi) + dot(hi, rg_lo))
+        if half_of:
+            far_copies[0].start()
     power[...] = jnp.zeros(power.shape, F32)
     box = column_box()
     for tile in range(NT):
         s0, s1 = both_parts(stacks, tile)
         add_columns(power, box, tile, s0 * s0 + s1 * s1)
+    for copy in far_copies:
+        copy.wait()
 
 
 def column_box():
@@ -190,16 +197,20 @@
         out_shape=tuple(space((rows, TILE), F32) for space in spaces)
         + (VMEM((LCOLS + 16, ROWS), F32),),
         in_specs=[pl.BlockSpec(memory_space=pl.ANY)] * 8,
-        out_specs=(pl.BlockSpec(memory_space=VMEM),) * (len(spaces) + 1),
+        out_specs=tuple(
+            pl.BlockSpec(memory_space=VMEM if space is VMEM else pl.ANY) for space in spaces
+        )
+        + (pl.BlockSpec(memory_space=VMEM),),
         scratch_shapes=[
             pltpu.VMEM((2, ROWS + 16, COLS), BF16),
             pltpu.VMEM((2, 2, 8, COLS), BF16),
             pltpu.VMEM((NT * 2 * ROWS, 2 * TILE), BF16),
             pltpu.VMEM((NT * 2 * ROWS, 2 * TILE), BF16),
-            pltpu.SemaphoreType.DMA((9,)),
+            pltpu.SemaphoreType.DMA((10,)),
         ]
         + [SMEM((2,), jnp.int32)] * 4
-        + [SMEM((KBANK, TAPS), F32)],
+        + [SMEM((KBANK, TAPS), F32)]
+        + [pltpu.VMEM((rows, TILE), F32)] * (len(spaces) - 1),
         cost_estimate=pl.CostEstimate(
             flops=3_000_000_000, transcendentals=0, bytes_accessed=1_600_000
         ),

time: 74.8 us -> 74.8 us (level)
  transfers between devices with their start and end apart: 14 -> 14, of which waited for: 5 -> 5; matrix products, arithmetic and copies ran while one was open for 0% -> 0% of each run, Pallas kernels for 11% -> 12%
where the time goes in v4:
time: 74.8 us; the launch traced here: 73.9 us
  starting transfers between devices  24.3 us (32%)
  waiting for transfers between devices  16.4 us (22%)
  blocking collectives  16.2 us (22%)
  Pallas kernels  15.1 us (20%)
  local copies, waits for them, and re-layouts  0.94 us (1%)
  between operations  0.9 us (1%)
    all_to_all x1, blocking collectives, body(): lax.all_to_all(outgoing, 'date', split_axis=0, concat_axis=0, tiled=True)  16.2 us
    ppermute x6, starting transfers between devices, send(): return lax.ppermute(value, ('date', 'az'), pairs)  10.5 us
    pallas_call x2, Pallas kernels, resample(): pl.pallas_call(functools.partial(resample_kernel, date, len(spaces)), com...  8.5 us
    all_to_all x1, waiting for transfers between devices, body(): lax.all_to_all(copies, 'date', 0, 0, axis_index_groups=planes, tiled=True)  7.67 us
    all_to_all x1, starting transfers between devices, body(): lax.all_to_all(copies, 'date', 0, 0, axis_index_groups=planes, tiled=True)  5.71 us
    ppermute x2, waiting for transfers between devices, swapped(): other = lax.ppermute(to_other, 'az', [(1, 2), (2, 1)])  5.07 us
    ppermute x2, starting transfers between devices, swapped(): other = lax.ppermute(to_other, 'az', [(1, 2), (2, 1)])  4.03 us
    ppermute x3, starting transfers between devices, body(): lax.ppermute(chunk, 'date', [(place(0, *home), place(k, *home)) for home...  3.88 us
  transfers between devices with their start and end apart: 14, of which 5 were waited for; matrix products, arithmetic and copies ran while one was open for 0% of the time, Pallas kernels for 12%

profile of v4, /device:TPU:32, one launch (start us, length us, event | category | flops | bytes accessed | tf_op | source)
XLA Modules:
  0.0 73.9 jit_solution(11665275680864764161)
XLA Ops:
  0.6 1.5 %quarters.1 = (bf16[4,8,3072]{2,1,0:T(8,128)(2,1)S(1)}, bf16[4,8,3072]{2,1,0:T(8,128)(2,1)S(1)}, bf16[4,8,3072]{2,1,0:T(8,128)(2,1)S(1)}, bf16[4,8,3072]{2,1,0:T...) custom-call(bf16[2,2,64,3072]{3,2,1,0:T(8,128)(2,1)} %refs_5_.3), custom_call_target="tpu_custom_call" | custom-call | tf_op jit(solution)/shard_map/quarters/pallas_call | solution.py:375
  2.2 3.4 %collective-permute-start = (bf16[4,8,3072]{2,1,0:T(8,128)(2,1)S(1)}, bf16[4,8,3072]{2,1,0:T(8,128)(2,1)S(1)}, u32[]{:S(2)}, u32[]{:S(2)}) collective-permute-start(bf16[4,8,3072]{2,1,0:T(8,128)(2,1)S(1)} %get-tuple-element.22), channel_id=1, source_target_pairs={{0,16},{1,13},{2,18},{3,15}} | collective-permute-start | bytes 589832 | tf_op jit(solution)/shard_map/ppermute | solution.py:430
  5.6 1.9 %collective-permute-start.1 = (bf16[4,8,3072]{2,1,0:T(8,128)(2,1)S(1)}, bf16[4,8,3072]{2,1,0:T(8,128)(2,1)S(1)}, u32[]{:S(2)}, u32[]{:S(2)}) collective-permute-start(bf16[4,8,3072]{2,1,0:T(8,128)(2,1)S(1)} %get-tuple-element.23), channel_id=1, source_target_pairs={{0,48},{1,5},{2,50},{3,7}} | collective-permute-start | bytes 589832 | tf_op jit(solution)/shard_map/ppermute | solution.py:430
  7.5 1.3 %collective-permute-start.2 = (bf16[4,8,3072]{2,1,0:T(8,128)(2,1)S(1)}, bf16[4,8,3072]{2,1,0:T(8,128)(2,1)S(1)}, u32[]{:S(2)}, u32[]{:S(2)}) collective-permute-start(bf16[4,8,3072]{2,1,0:T(8,128)(2,1)S(1)} %get-tuple-element.24), channel_id=1, source_target_pairs={{0,4},{1,17},{2,6},{3,19}} | collective-permute-start | bytes 589832 | tf_op jit(solution)/shard_map/ppermute | solution.py:430
  8.9 1.8 %collective-permute-done.1 = bf16[4,8,3072]{2,1,0:T(8,128)(2,1)S(1)} collective-permute-done((bf16[4,8,3072]{2,1,0:T(8,128)(2,1)S(1)}, bf16[4,8,3072]{2,1,0:T(8,128)(2,1)S(1)}, u32[]{:S(2)}, u32[]{:S(2)}) %collective-permute-start.1) | collective-permute-done | bytes 196640 | tf_op jit(solution)/shard_map/ppermute | solution.py:430
  10.7 1.9 %collective-permute-done.2 = bf16[4,8,3072]{2,1,0:T(8,128)(2,1)S(1)} collective-permute-done((bf16[4,8,3072]{2,1,0:T(8,128)(2,1)S(1)}, bf16[4,8,3072]{2,1,0:T(8,128)(2,1)S(1)}, u32[]{:S(2)}, u32[]{:S(2)}) %collective-permute-start.2) | collective-permute-done | bytes 196640 | tf_op jit(solution)/shard_map/ppermute | solution.py:430
  12.6 1.3 %collective-permute-start.4 = (bf16[1,8,3072]{2,1,0:T(8,128)(2,1)S(1)}, bf16[1,8,3072]{2,1,0:T(8,128)(2,1)S(1)}, u32[]{:S(2)}, u32[]{:S(2)}) collective-permute-start(bf16[1,8,3072]{2,1,0:T(8,128)(2,1)S(1)} %get-tuple-element.40), channel_id=1, source_target_pairs={{0,28},{16,20},{48,56},{4,24},{1,61},{13,29},{5,37},{17,45},{2,30}... | collective-permute-start | bytes 147464 | tf_op jit(solution)/shard_map/ppermute | solution.py:430
  13.9 1.3 %collective-permute-start.5 = (bf16[1,8,3072]{2,1,0:T(8,128)(2,1)S(1)}, bf16[1,8,3072]{2,1,0:T(8,128)(2,1)S(1)}, u32[]{:S(2)}, u32[]{:S(2)}) collective-permute-start(bf16[1,8,3072]{2,1,0:T(8,128)(2,1)S(1)} %get-tuple-element.41), channel_id=1, source_target_pairs={{0,60},{16,36},{48,44},{4,40},{1,53},{13,25},{5,57},{17,41},{2,62}... | collective-permute-start | bytes 147464 | tf_op jit(solution)/shard_map/ppermute | solution.py:430
  15.2 1.3 %collective-permute-start.3 = (bf16[1,8,3072]{2,1,0:T(8,128)(2,1)S(1)}, bf16[1,8,3072]{2,1,0:T(8,128)(2,1)S(1)}, u32[]{:S(2)}, u32[]{:S(2)}) collective-permute-start(bf16[1,8,3072]{2,1,0:T(8,128)(2,1)S(1)} %get-tuple-element.42), channel_id=1, source_target_pairs={{0,12},{16,32},{48,52},{4,8},{1,49},{13,9},{5,21},{17,33},{2,14},{... | collective-permute-start | bytes 147464 | tf_op jit(solution)/shard_map/ppermute | solution.py:430
  16.6 2.1 %collective-permute-start.10 = (bf16[2,2,8,3072]{3,2,1,0:T(8,128)(2,1)S(1)}, bf16[2,2,8,3072]{3,2,1,0:T(8,128)(2,1)S(1)}, u32[]{:S(2)}, u32[]{:S(2)}) collective-permute-start(bf16[2,2,8,3072]{3,2,1,0:T(8,128)(2,1)S(1)} %get-tuple-element.26), channel_id=1, source_target_pairs={{1,2},{2,1},{5,6},{6,5},{9,10},{10,9},{13,14},{14,13},{17,18},{18,... | collective-permute-start | bytes 589832 | tf_op jit(solution)/shard_map/ppermute | solution.py:78
  18.8 1.3 %collective-permute-start.8 = (bf16[1,8,3072]{2,1,0:T(8,128)(2,1)S(1)}, bf16[1,8,3072]{2,1,0:T(8,128)(2,1)S(1)}, u32[]{:S(2)}, u32[]{:S(2)}) collective-permute-start(bf16[1,8,3072]{2,1,0:T(8,128)(2,1)S(1)} %slice_add_fusion.own), channel_id=1, source_target_pairs={{0,128},{12,140},{28,156},{60,188},{16,144},{32,160},{20,148},{36,... | collective-permute-start | bytes 147464 | tf_op jit(solution)/shard_map/ppermute | solution.py:457
  20.1 1.3 %collective-permute-start.7 = (bf16[1,8,3072]{2,1,0:T(8,128)(2,1)S(1)}, bf16[1,8,3072]{2,1,0:T(8,128)(2,1)S(1)}, u32[]{:S(2)}, u32[]{:S(2)}) collective-permute-start(bf16[1,8,3072]{2,1,0:T(8,128)(2,1)S(1)} %slice_add_fusion.own), channel_id=1, source_target_pairs={{0,192},{12,204},{28,220},{60,252},{16,208},{32,224},{20,212},{36,... | collective-permute-start | bytes 147464 | tf_op jit(solution)/shard_map/ppermute | solution.py:457
  21.4 1.3 %collective-permute-start.6 = (bf16[1,8,3072]{2,1,0:T(8,128)(2,1)S(1)}, bf16[1,8,3072]{2,1,0:T(8,128)(2,1)S(1)}, u32[]{:S(2)}, u32[]{:S(2)}) collective-permute-start(bf16[1,8,3072]{2,1,0:T(8,128)(2,1)S(1)} %slice_add_fusion.own), channel_id=1, source_target_pairs={{0,64},{12,76},{28,92},{60,124},{16,80},{32,96},{20,84},{36,100},{... | collective-permute-start | bytes 147464 | tf_op jit(solution)/shard_map/ppermute | solution.py:457
  22.7 1.2 %collective-permute-done.10.refs_7_ = bf16[2,2,8,3072]{3,2,1,0:T(8,128)(2,1)S(1)} collective-permute-done((bf16[2,2,8,3072]{3,2,1,0:T(8,128)(2,1)S(1)}, bf16[2,2,8,3072]{3,2,1,0:T(8,128)(2,1)S(1)}, u32[]{:S(2)}, u32[]{:S(2)}) %collective-permute-start.10) | collective-permute-done | bytes 196640 | tf_op jit(solution)/shard_map/ppermute | solution.py:78
  23.9 4.5 %shard_map.77 = (f32[768,256]{1,0:T(8,128)S(1)}, f32[768,256]{1,0:T(8,128)}, f32[208,64]{1,0:T(8,128)S(1)}) custom-call(s32[2]{0:T(128)} %refs_0_.3, s32[2]{0:T(128)} %refs_1_.3, s32[2]{0:T(128)} %refs_2_.3, s32[2]{0:T(128)} %refs_3_.3, f32[16,8]{1,0:T(8,128)} %constant.12.clone.refs_4_, bf16[2,2,64,3072]{3,2,1,0:T(8,128)(2,1)} %refs_5_.3, ...), custom_call_target="tpu_custom_call" | custom-call | flops 3000000000 | bytes 1600000 | tf_op jit(solution)/shard_map/pallas_call | solution.py:194
  28.4 1.1 %copies.1 = bf16[16,8,3072]{2,1,0:T(8,128)(2,1)} custom-call(bf16[1,8,3072]{2,1,0:T(8,128)(2,1)S(1)} %slice_add_fusion.own, bf16[1,8,3072]{2,1,0:T(8,128)(2,1)S(1)} %collective-permute-done.6.rest_0_, bf16[1,8,3072]{2,1,0:T(8,128)(2,1)S(1)} %collective-permute-done.7.rest_1_, bf16[1,8,3072]{2,1,0:T(8,128)(2,1)S(1)} %collective-permute-done.8.rest_2_), custom_call_target="tpu_custom_call" | custom-call | tf_op jit(solution)/shard_map/copies/pallas_call | solution.py:400
  29.5 5.7 %all-to-all-start = ((bf16[16,8,3072]{2,1,0:T(8,128)(2,1)}), bf16[16,8,3072]{2,1,0:T(8,128)(2,1)S(1)}, u32[]{:S(2)}, u32[]{:S(2)}) async-start(bf16[16,8,3072]{2,1,0:T(8,128)(2,1)} %copies.1), calls=%async_computation | async-start | bytes 1572864 | tf_op jit(solution)/shard_map/all_to_all | solution.py:465
  36.1 4.0 %shard_map.78 = (f32[1536,256]{1,0:T(8,128)S(1)}, f32[208,64]{1,0:T(8,128)S(1)}) custom-call(s32[2]{0:T(128)} %refs_0_.3, s32[2]{0:T(128)} %refs_1_.3, s32[2]{0:T(128)} %refs_2_.3, s32[2]{0:T(128)} %refs_3_.3, f32[16,8]{1,0:T(8,128)} %constant.12.clone.refs_4_, bf16[2,2,64,3072]{3,2,1,0:T(8,128)(2,1)} %refs_5_.3, ...), custom_call_target="tpu_custom_call" | custom-call | flops 3000000000 | bytes 1600000 | tf_op jit(solution)/shard_map/pallas_call | solution.py:194
  40.2 7.7 %all-to-all-done.center = bf16[16,8,3072]{2,1,0:T(8,128)(2,1)S(1)} async-done(((bf16[16,8,3072]{2,1,0:T(8,128)(2,1)}), bf16[16,8,3072]{2,1,0:T(8,128)(2,1)S(1)}, u32[]{:S(2)}, u32[]{:S(2)}) %all-to-all-start) | async-done | bytes 786464 | tf_op jit(solution)/shard_map/all_to_all | solution.py:465
  47.8 2.1 %looks.1.own = f32[192,128]{1,0:T(8,128)S(1)} custom-call(bf16[16,8,3072]{2,1,0:T(8,128)(2,1)S(1)} %all-to-all-done.center, f32[768,256]{1,0:T(8,128)S(1)} %get-tuple-element.33.near_first, f32[1536,256]{1,0:T(8,128)S(1)} %get-tuple-element.34.second, f32[208,64]{1,0:T(8,128)S(1)} %get-tuple-element.35.power0, f32[208,64]{1,0:T(8,128)S(1)} %get-tuple-element.36.power1, ...), custom_call_target="tpu_custom_call" | custom-call | tf_op jit(solution)/shard_map/looks/pallas_call | solution.py:254
  49.9 1.9 %collective-permute-start.12 = (f32[192,128]{1,0:T(8,128)S(1)}, f32[192,128]{1,0:T(8,128)S(1)}, u32[]{:S(2)}, u32[]{:S(2)}) collective-permute-start(f32[192,128]{1,0:T(8,128)S(1)} %looks.1.own), channel_id=1, source_target_pairs={{1,2},{2,1},{5,6},{6,5},{9,10},{10,9},{13,14},{14,13},{17,18},{18,... | collective-permute-start | bytes 294920 | tf_op jit(solution)/shard_map/ppermute | solution.py:78
  51.9 3.9 %collective-permute-done.12.other = f32[192,128]{1,0:T(8,128)S(1)} collective-permute-done((f32[192,128]{1,0:T(8,128)S(1)}, f32[192,128]{1,0:T(8,128)S(1)}, u32[]{:S(2)}, u32[]{:S(2)}) %collective-permute-start.12) | collective-permute-done | bytes 98336 | tf_op jit(solution)/shard_map/ppermute | solution.py:78
  56.4 16.2 %all_to_all.10.arrived = bf16[64,2,128]{2,1,0:T(2,128)(2,1)S(1)} all-to-all(bf16[64,2,128]{2,1,0:T(2,128)(2,1)S(1)} %coherence.1), channel_id=1, replica_groups=mesh['date'=64,'az'=4] {'date'}, dimensions={0} | all-to-all | bytes 65536 | tf_op jit(solution)/shard_map/all_to_all | solution.py:471
  72.6 1.3 %finish.1 = (bf16[96,128]{1,0:T(8,128)(2,1)}, f32[3,16]{1,0:T(4,128)}) custom-call(bf16[64,2,128]{2,1,0:T(2,128)(2,1)S(1)} %all_to_all.10.arrived), custom_call_target="tpu_custom_call" | custom-call | tf_op jit(solution)/shard_map/finish/pallas_call | solution.py:338
  (20 shorter events, 1.8 us)
Async XLA Ops:
  2.2 6.7 %collective-permute-start = (bf16[4,8,3072]{2,1,0:T(8,128)(2,1)S(1)}, bf16[4,8,3072]{2,1,0:T(8,128)(2,1)S(1)}, u32[]{:S(2)}, u32[]{:S(2)}) collective-permute-start(bf16[4,8,3072]{2,1,0:T(8,128)(2,1)S(1)} %get-tuple-element.22), channel_id=1, source_target_pairs={{0,16},{1,13},{2,18},{3,15}} | collective-permute-start | bytes 589832 | tf_op jit(solution)/shard_map/ppermute | solution.py:430
  5.6 5.1 %collective-permute-start.1 = (bf16[4,8,3072]{2,1,0:T(8,128)(2,1)S(1)}, bf16[4,8,3072]{2,1,0:T(8,128)(2,1)S(1)}, u32[]{:S(2)}, u32[]{:S(2)}) collective-permute-start(bf16[4,8,3072]{2,1,0:T(8,128)(2,1)S(1)} %get-tuple-element.23), channel_id=1, source_target_pairs={{0,48},{1,5},{2,50},{3,7}} | collective-permute-start | bytes 589832 | tf_op jit(solution)/shard_map/ppermute | solution.py:430
  7.5 5.0 %collective-permute-start.2 = (bf16[4,8,3072]{2,1,0:T(8,128)(2,1)S(1)}, bf16[4,8,3072]{2,1,0:T(8,128)(2,1)S(1)}, u32[]{:S(2)}, u32[]{:S(2)}) collective-permute-start(bf16[4,8,3072]{2,1,0:T(8,128)(2,1)S(1)} %get-tuple-element.24), channel_id=1, source_target_pairs={{0,4},{1,17},{2,6},{3,19}} | collective-permute-start | bytes 589832 | tf_op jit(solution)/shard_map/ppermute | solution.py:430
  12.6 6.1 %collective-permute-start.4 = (bf16[1,8,3072]{2,1,0:T(8,128)(2,1)S(1)}, bf16[1,8,3072]{2,1,0:T(8,128)(2,1)S(1)}, u32[]{:S(2)}, u32[]{:S(2)}) collective-permute-start(bf16[1,8,3072]{2,1,0:T(8,128)(2,1)S(1)} %get-tuple-element.40), channel_id=1, source_target_pairs={{0,28},{16,20},{48,56},{4,24},{1,61},{13,29},{5,37},{17,45},{2,30}... | collective-permute-start | bytes 147464 | tf_op jit(solution)/shard_map/ppermute | solution.py:430
  13.9 4.8 %collective-permute-start.5 = (bf16[1,8,3072]{2,1,0:T(8,128)(2,1)S(1)}, bf16[1,8,3072]{2,1,0:T(8,128)(2,1)S(1)}, u32[]{:S(2)}, u32[]{:S(2)}) collective-permute-start(bf16[1,8,3072]{2,1,0:T(8,128)(2,1)S(1)} %get-tuple-element.41), channel_id=1, source_target_pairs={{0,60},{16,36},{48,44},{4,40},{1,53},{13,25},{5,57},{17,41},{2,62}... | collective-permute-start | bytes 147464 | tf_op jit(solution)/shard_map/ppermute | solution.py:430
  15.2 3.5 %collective-permute-start.3 = (bf16[1,8,3072]{2,1,0:T(8,128)(2,1)S(1)}, bf16[1,8,3072]{2,1,0:T(8,128)(2,1)S(1)}, u32[]{:S(2)}, u32[]{:S(2)}) collective-permute-start(bf16[1,8,3072]{2,1,0:T(8,128)(2,1)S(1)} %get-tuple-element.42), channel_id=1, source_target_pairs={{0,12},{16,32},{48,52},{4,8},{1,49},{13,9},{5,21},{17,33},{2,14},{... | collective-permute-start | bytes 147464 | tf_op jit(solution)/shard_map/ppermute | solution.py:430
  16.5 6.2 %collective-permute-start.9 = (bf16[2,2,8,3072]{3,2,1,0:T(8,128)(2,1)S(1)}, bf16[2,2,8,3072]{3,2,1,0:T(8,128)(2,1)S(1)}, u32[]{:S(2)}, u32[]{:S(2)}) collective-permute-start(bf16[2,2,8,3072]{3,2,1,0:T(8,128)(2,1)S(1)} %get-tuple-element.25), channel_id=1, source_target_pairs={{0,1},{1,0},{2,3},{3,2},{4,5},{5,4},{6,7},{7,6},{8,9},{9,8},{10,11... | collective-permute-start | bytes 589832 | tf_op jit(solution)/shard_map/ppermute | solution.py:77
  16.6 7.2 %collective-permute-start.10 = (bf16[2,2,8,3072]{3,2,1,0:T(8,128)(2,1)S(1)}, bf16[2,2,8,3072]{3,2,1,0:T(8,128)(2,1)S(1)}, u32[]{:S(2)}, u32[]{:S(2)}) collective-permute-start(bf16[2,2,8,3072]{3,2,1,0:T(8,128)(2,1)S(1)} %get-tuple-element.26), channel_id=1, source_target_pairs={{1,2},{2,1},{5,6},{6,5},{9,10},{10,9},{13,14},{14,13},{17,18},{18,... | collective-permute-start | bytes 589832 | tf_op jit(solution)/shard_map/ppermute | solution.py:78
  18.8 9.6 %collective-permute-start.8 = (bf16[1,8,3072]{2,1,0:T(8,128)(2,1)S(1)}, bf16[1,8,3072]{2,1,0:T(8,128)(2,1)S(1)}, u32[]{:S(2)}, u32[]{:S(2)}) collective-permute-start(bf16[1,8,3072]{2,1,0:T(8,128)(2,1)S(1)} %slice_add_fusion.own), channel_id=1, source_target_pairs={{0,128},{12,140},{28,156},{60,188},{16,144},{32,160},{20,148},{36,... | collective-permute-start | bytes 147464 | tf_op jit(solution)/shard_map/ppermute | solution.py:457
  20.1 8.3 %collective-permute-start.7 = (bf16[1,8,3072]{2,1,0:T(8,128)(2,1)S(1)}, bf16[1,8,3072]{2,1,0:T(8,128)(2,1)S(1)}, u32[]{:S(2)}, u32[]{:S(2)}) collective-permute-start(bf16[1,8,3072]{2,1,0:T(8,128)(2,1)S(1)} %slice_add_fusion.own), channel_id=1, source_target_pairs={{0,192},{12,204},{28,220},{60,252},{16,208},{32,224},{20,212},{36,... | collective-permute-start | bytes 147464 | tf_op jit(solution)/shard_map/ppermute | solution.py:457
  21.4 7.0 %collective-permute-start.6 = (bf16[1,8,3072]{2,1,0:T(8,128)(2,1)S(1)}, bf16[1,8,3072]{2,1,0:T(8,128)(2,1)S(1)}, u32[]{:S(2)}, u32[]{:S(2)}) collective-permute-start(bf16[1,8,3072]{2,1,0:T(8,128)(2,1)S(1)} %slice_add_fusion.own), channel_id=1, source_target_pairs={{0,64},{12,76},{28,92},{60,124},{16,80},{32,96},{20,84},{36,100},{... | collective-permute-start | bytes 147464 | tf_op jit(solution)/shard_map/ppermute | solution.py:457
  23.9 4.5 %copy-start = (bf16[2,2,8,3072]{3,2,1,0:T(8,128)(2,1)}, bf16[2,2,8,3072]{3,2,1,0:T(8,128)(2,1)S(1)}, u32[]{:S(2)}) copy-start(bf16[2,2,8,3072]{3,2,1,0:T(8,128)(2,1)S(1)} %collective-permute-done.10.refs_7_) | copy-start | bytes 589828
  29.5 18.3 %all-to-all-start = ((bf16[16,8,3072]{2,1,0:T(8,128)(2,1)}), bf16[16,8,3072]{2,1,0:T(8,128)(2,1)S(1)}, u32[]{:S(2)}, u32[]{:S(2)}) async-start(bf16[16,8,3072]{2,1,0:T(8,128)(2,1)} %copies.1), calls=%async_computation | async-start | bytes 1572864 | tf_op jit(solution)/shard_map/all_to_all | solution.py:465
  35.2 0.9 %copy-start.1 = (bf16[2,2,8,3072]{3,2,1,0:T(8,128)(2,1)S(1)}, bf16[2,2,8,3072]{3,2,1,0:T(8,128)(2,1)}, u32[]{:S(2)}) copy-start(bf16[2,2,8,3072]{3,2,1,0:T(8,128)(2,1)} %copy-done) | copy-start | bytes 589828
  49.9 5.9 %collective-permute-start.12 = (f32[192,128]{1,0:T(8,128)S(1)}, f32[192,128]{1,0:T(8,128)S(1)}, u32[]{:S(2)}, u32[]{:S(2)}) collective-permute-start(f32[192,128]{1,0:T(8,128)S(1)} %looks.1.own), channel_id=1, source_target_pairs={{1,2},{2,1},{5,6},{6,5},{9,10},{10,9},{13,14},{14,13},{17,18},{18,... | collective-permute-start | bytes 294920 | tf_op jit(solution)/shard_map/ppermute | solution.py:78
  51.8 4.0 %collective-permute-start.11 = (f32[192,128]{1,0:T(8,128)S(1)}, f32[192,128]{1,0:T(8,128)S(1)}, u32[]{:S(2)}, u32[]{:S(2)}) collective-permute-start(f32[192,128]{1,0:T(8,128)S(1)} %looks.1.own), channel_id=1, source_target_pairs={{0,1},{1,0},{2,3},{3,2},{4,5},{5,4},{6,7},{7,6},{8,9},{9,8},{10,11... | collective-permute-start | bytes 294920 | tf_op jit(solution)/shard_map/ppermute | solution.py:77
